TPU v7x, 32 devices: a whole 2x2x4 slice. The times are simulated.
32 devices in a mesh: section: 8 (over y, x, core), ctx: 4 (over z).
Axes of the slice: x: 2, y: 2, z: 4, core: 2. Of those that a mesh axis runs over, the one named last changes fastest.
Arguments:
- section_inputs: bfloat16 [8, 448, 2048], P('section', 'ctx'), may hold values from -3 to 3
- saved_inputs: bfloat16 [8, 448, 2048], P('section', 'ctx'), may hold values from -3 to 3
- output_grads: bfloat16 [8, 448, 2048], P('section', 'ctx'), may hold values from -6 to 6
- token_positions: int32 [448], P('ctx'), may hold values from 0 to 447, each once
- norm_gain: float32 [8, 2048], P('section'), may hold values from 0.7 to 6
- query_weight: bfloat16 [8, 2048, 2048], P('section', 'ctx'), may hold values from -0.13258252 to 0.13258252
- keyval_weight: bfloat16 [8, 2048, 1024], P('section', 'ctx'), may hold values from -0.13258252 to 0.13258252
- output_weight: bfloat16 [8, 2048, 2048], P('section'), may hold values from -0.125 to 0.125
Outputs:
- next_inputs: bfloat16 [8, 448, 2048], P('section', 'ctx')
- input_grads: bfloat16 [8, 448, 2048], P('section', 'ctx')
Inputs may be any that keep to these rules, and one draw needn't show every extreme that they name: `token_positions`: each position of the sequence once.
All inputs are finite; a program needn't handle non-finite values.
Results may differ from a plain program's by a relative error of at most 0.04.
The roundings to bfloat16 on the way count: a program that leaves them out, or rounds other values in their place, can miss the bound.
Values may be sent and summed in bfloat16 or wider, within the bound.
A program may use at most 192 MiB of HBM per device.

v0:
```python
import functools

import jax
import jax.numpy as jnp
import numpy as np
from jax import lax
from jax.experimental import pallas as pl
from jax.experimental.pallas import tpu as pltpu
from jax.sharding import PartitionSpec as P

HEAD_DIM = 128


norm_eps = 1e-05
rope_base = 500000.0


def from_behind(block, axis, distance):
    devices = range(lax.axis_size(axis))
    route = [((i - distance) % len(devices), i) for i in devices]
    return lax.ppermute(block, axis, route)


def rotate(matrix, positions):
    half_dim = matrix.shape[-1] // 2
    frequency = rope_base ** (-2.0 * jnp.arange(half_dim, dtype=jnp.float32) / matrix.shape[-1])
    angles = positions.astype(jnp.float32)[:, None] * frequency[None, :]
    cos_table = jnp.cos(angles)[:, None, :]
    sin_table = jnp.sin(angles)[:, None, :]
    leading = matrix[..., :half_dim]
    trailing = matrix[..., half_dim:]
    return jnp.concatenate(
        [leading * cos_table - trailing * sin_table, trailing * cos_table + leading * sin_table],
        axis=-1,
    )


def project(tokens, gain, query_matrix, keyval_matrix, positions):
    widened = tokens.astype(jnp.float32)
    inverse = lax.rsqrt(jnp.mean(widened * widened, axis=-1, keepdims=True) + norm_eps)
    normed = (widened * inverse * gain[None, :]).astype(jnp.bfloat16)
    row_count = tokens.shape[0]
    query_full = jnp.dot(normed, query_matrix, preferred_element_type=jnp.float32)
    keyval_full = jnp.dot(normed, keyval_matrix, preferred_element_type=jnp.float32)
    queries = rotate(query_full.reshape(row_count, -1, HEAD_DIM), positions).astype(jnp.bfloat16)
    paired = keyval_full.reshape(row_count, 2, -1, HEAD_DIM)
    key_rows = rotate(paired[:, 0], positions).astype(jnp.bfloat16)
    value_rows = paired[:, 1].astype(jnp.bfloat16)
    return (queries, key_rows, value_rows)


def attend(queries, key_wide, value_wide, query_pos, key_pos, narrow):
    row_count = queries.shape[0]
    kv_count = key_wide.shape[1]
    head_size = queries.shape[2]
    group_size = queries.shape[1] // kv_count
    grouped = jnp.moveaxis(queries.reshape(row_count, kv_count, group_size, head_size), 1, 0)
    key_heads = jnp.moveaxis(key_wide, 1, 0)
    value_heads = jnp.moveaxis(value_wide, 1, 0)
    visible = (key_pos[None, :] <= query_pos[:, None])[None]

    def one_head(block):
        query_block, key_block, value_block = block
        scores = jnp.einsum(
            "rgd,sd->grs", query_block, key_block, preferred_element_type=jnp.float32
        ) * head_size ** (-0.5)
        masked = jnp.where(visible, scores, -1e30)
        row_max = lax.stop_gradient(jnp.max(masked, axis=-1, keepdims=True))
        numerators = jnp.where(visible, jnp.exp(masked - row_max), 0.0)
        totals = jnp.sum(numerators, axis=-1)
        if narrow:
            rounded = numerators.astype(jnp.bfloat16)
        else:
            rounded = lax.optimization_barrier(numerators.astype(jnp.bfloat16)).astype(jnp.float32)
        summed = jnp.einsum("grs,sd->rgd", rounded, value_block, preferred_element_type=jnp.float32)
        return summed / jnp.transpose(totals, (1, 0))[..., None]

    averaged = lax.map(one_head, (grouped, key_heads, value_heads))
    return jnp.moveaxis(averaged, 0, 1).reshape(row_count, -1).astype(jnp.bfloat16)


def finish(tokens, mixed, output_matrix):
    return (
        tokens.astype(jnp.float32)
        + jnp.dot(mixed, output_matrix, preferred_element_type=jnp.float32)
    ).astype(jnp.bfloat16)


def shards(
    section_inputs,
    saved_inputs,
    output_grads,
    token_positions,
    norm_gain,
    query_weight,
    keyval_weight,
    output_weight,
):
    key_positions = lax.all_gather(token_positions, "ctx", axis=0, tiled=True)
    full_query, full_keyval = (
        lax.all_gather(query_weight[0], "ctx", axis=0, tiled=True),
        lax.all_gather(keyval_weight[0], "ctx", axis=0, tiled=True),
    )
    full_output = output_weight[0]
    gain = norm_gain[0]
    forward_tokens = section_inputs[0]
    saved_tokens = saved_inputs[0]
    upstream = output_grads[0]

    def projector(tokens):
        return project(tokens, gain, full_query, full_keyval, token_positions)

    def attention_wide(queries, key_wide, value_wide):
        return attend(queries, key_wide, value_wide, token_positions, key_positions, False)

    def finishing(tokens, mixed):
        return finish(tokens, mixed, full_output)

    forward_queries, forward_keys, forward_values = projector(forward_tokens)
    (backward_queries, backward_keys, backward_values), back_project = jax.vjp(
        projector, saved_tokens
    )
    forward_keyset, forward_valueset = (
        lax.all_gather(forward_keys, "ctx", axis=0, tiled=True),
        lax.all_gather(forward_values, "ctx", axis=0, tiled=True),
    )
    mixed = attend(
        forward_queries, forward_keyset, forward_valueset, token_positions, key_positions, True
    )
    produced = finishing(forward_tokens, mixed)
    sent_on = from_behind(produced[None], "section", 1)
    backward_keyset, backward_valueset = (
        lax.all_gather(backward_keys, "ctx", axis=0, tiled=True),
        lax.all_gather(backward_values, "ctx", axis=0, tiled=True),
    )
    mixed, back_attend = jax.vjp(
        attention_wide,
        backward_queries.astype(jnp.float32),
        backward_keyset.astype(jnp.float32),
        backward_valueset.astype(jnp.float32),
    )
    produced, back_finish = jax.vjp(finishing, saved_tokens, mixed)
    residual_grad, mixed_grad = back_finish(upstream)
    query_grad, key_partial, value_partial = back_attend(mixed_grad)
    key_grads = lax.psum_scatter(
        key_partial.astype(jnp.bfloat16), "ctx", scatter_dimension=0, tiled=True
    )
    value_grads = lax.psum_scatter(
        value_partial.astype(jnp.bfloat16), "ctx", scatter_dimension=0, tiled=True
    )
    (project_grad,) = back_project((query_grad.astype(jnp.bfloat16), key_grads, value_grads))
    sent_back = from_behind((residual_grad + project_grad)[None], "section", -1)
    return (sent_on, sent_back)


MESH = pl.DeviceIdType.MESH
VMEM = pl.BlockSpec(memory_space=pltpu.VMEM)
ANY = pl.BlockSpec(memory_space=pl.ANY)
WIDE = jnp.float32
SLIM = jnp.bfloat16


def remote(src, dst, send, recv, device):
    return pltpu.make_async_remote_copy(
        src_ref=src, dst_ref=dst, send_sem=send, recv_sem=recv, device_id=device, device_id_type=MESH
    )


def layer_kernel(
    n, sections, nf, nb, up, wo_hbm, wq, wkv, pos, waves, tokens, saved, gain, ahead, back,
    xf, xb, mgl, mg, wo, wh, posg, qcol, cos, sin, qkv_f, qkv_b, mixed, dqkv, mixed_in, part, inbox,
    produced, grads, fsend, frecv, gsend, grecv, wsend, wrecv, msend, mrecv, psend, precv,
    asend, arecv, bsend, brecv, csend, crecv, own,
):
    section = lax.axis_index("section")
    me = lax.axis_index("ctx")
    depth, _ = wq.shape
    rows, gq = mg.shape[1:]
    wide = wh.shape[2]
    kvw = (wide - gq) // 2
    half = kvw * n
    group = gq // kvw
    scale = HEAD_DIM ** (-0.5)
    following, preceding = lax.rem(section + 1, sections), lax.rem(section + sections - 1, sections)

    barrier = pltpu.get_barrier_semaphore()
    for k in range(1, n):
        pl.semaphore_signal(barrier, inc=1, device_id=(section, lax.rem(me + k, n)), device_id_type=MESH)
    for other in (following, preceding):
        pl.semaphore_signal(barrier, inc=1, device_id=(other, me), device_id_type=MESH)
    pl.semaphore_wait(barrier, n + 1)

    def peer(side, t):
        return (me + t, me + t < n) if side == 0 else (me - t, me - t >= 0)

    def behind(side, t):
        return peer(1 - side, t)

    def begin(copies):
        for copy in copies:
            copy.start()

    def arrive(copies):
        for copy in copies:
            copy.wait_recv()

    def leave(copies):
        for copy in copies:
            copy.wait_send()

    def weight_copies(side, t, target, source):
        parts = (
            (wq, target * gq, gq, 0),
            (wkv, target * kvw, kvw, gq),
            (wkv, half + target * kvw, kvw, gq + kvw),
        )
        return [
            remote(
                ref.at[:, pl.ds(pl.multiple_of(start, 128), size)],
                wh.at[source, :, pl.ds(to, size)],
                wsend.at[side, t, i], wrecv.at[side, t, i], (section, target),
            )
            for i, (ref, start, size, to) in enumerate(parts)
        ]

    relays = ((nf, xf, fsend, frecv), (nb, xb, gsend, grecv))

    def row_copies(batch, side, t, block, target):
        first, every, send, recv = relays[batch]
        return [
            remote(
                first if t == 1 else every.at[block], every.at[block],
                send.at[side, t], recv.at[side, t], (section, target),
            )
        ]

    def small_copies(side, t, target):
        return [remote(mgl.at[target], mg.at[me], msend.at[side, t], mrecv.at[side, t], (section, target))]

    def place_copies(side, t, target):
        return [remote(pos, posg.at[me], psend.at[side, t], precv.at[side, t], (section, target))]

    def mixed_copies(side, t, target):
        return [
            remote(mixed.at[target], mixed_in.at[me], asend.at[side, t], arecv.at[side, t], (section, target))
        ]

    def hop(batch, side, t):
        block, there = behind(side, t)
        target, fits = peer(side, 1)
        pl.when(there)(lambda: arrive(row_copies(batch, side, t, block, me)))
        if t + 1 < n:
            pl.when(jnp.logical_and(there, fits))(
                lambda: begin(row_copies(batch, side, t + 1, block, target))
            )

    def send_own(batch):
        for side in (0, 1):
            target, fits = peer(side, 1)
            pl.when(fits)(lambda: begin(row_copies(batch, side, 1, me, target)))

    def to_all(copies, action):
        for t in range(n - 1, 0, -1):
            for side in (0, 1):
                target, fits = peer(side, t)
                pl.when(fits)(lambda: action(copies(side, t, target)))

    def from_all(copies):
        for t in range(1, n):
            for side in (0, 1):
                _, there = behind(side, t)
                pl.when(there)(lambda: arrive(copies(side, t, me)))

    send_own(0)
    send_own(1)
    to_all(place_copies, begin)
    wo_copy = pltpu.make_async_copy(wo_hbm, wo, own.at[0])
    wo_copy.start()
    mine = [
        pltpu.make_async_copy(
            ref.at[:, pl.ds(pl.multiple_of(start, 128), size)], wh.at[me, :, pl.ds(to, size)], own.at[i + 1]
        )
        for i, (ref, start, size, to) in enumerate(
            ((wq, me * gq, gq, 0), (wkv, me * kvw, kvw, gq), (wkv, half + me * kvw, kvw, gq + kvw))
        )
    ]
    begin(mine)
    posg[me] = pos[...]
    xf[me] = nf[...]
    xb[me] = nb[...]

    def send_weights(side):
        for t in range(n - 1, 0, -1):
            target, fits = peer(side, t)
            pl.when(fits)(lambda: begin(weight_copies(side, t, target, me)))

    for t in range(1, n):
        pl.when(me == t - 1)(lambda: send_weights(0))
        pl.when(n - me == t)(lambda: send_weights(1))
        for batch in (0, 1):
            for side in (0, 1):
                hop(batch, side, t)

    wo_copy.wait()
    for j in range(n):
        mgl[j] = lax.dot_general(
            up[...], wo[pl.ds(j * gq, gq), :], (((1,), (1,)), ((), ())), preferred_element_type=WIDE
        ).astype(SLIM)
    mg[me] = mgl[me]
    to_all(small_copies, begin)

    from_all(place_copies)
    for j in range(n):
        column = jnp.transpose(jnp.broadcast_to(posg[j].astype(WIDE), (HEAD_DIM, rows)))
        angles = column * waves[0:1, :]
        qcol[j] = column
        cos[pl.ds(j * rows, rows), :] = jnp.cos(angles)
        sin[pl.ds(j * rows, rows), :] = jnp.sin(angles) * waves[1:2, :]

    tile = 256 if wide % 256 == 0 else 128

    def add_from(j, first):
        columns = pl.ds(pl.multiple_of(j * depth, 128), depth)

        @pl.loop(0, wide // tile)
        def _(c):
            at = pl.ds(pl.multiple_of(c * tile, 128), tile)
            for every, total in ((xf, qkv_f), (xb, qkv_b)):
                term = jnp.dot(
                    every[:, :, columns].reshape(-1, depth), wh[j, :, at], preferred_element_type=WIDE
                )
                total[:, at] = term if first else total[:, at] + term

    for copy in mine:
        copy.wait()
    add_from(me, True)
    for t in range(1, n):
        for side in (0, 1):
            block, there = behind(side, t)

            @pl.when(there)
            def _():
                arrive(weight_copies(side, t, me, block))
                add_from(block, False)

    column = qcol[...].reshape(n * rows, HEAD_DIM)
    visible = jnp.transpose(column)[0:1, :] <= column[:, 0:1]

    def turn(block, sign):
        return block * cos[...] + sign * (pltpu.roll(block, HEAD_DIM // 2, 1) * sin[...])

    def dot(a, b, dims):
        return lax.dot_general(a, b, (dims, ((), ())), preferred_element_type=WIDE)

    def weigh(queries, keys):
        scores = dot(queries, keys, ((1,), (1,))) * scale
        masked = jnp.where(visible, scores, -1e30)
        row_max = jnp.max(masked, axis=-1, keepdims=True)
        numerators = jnp.where(visible, jnp.exp(masked - row_max), 0.0)
        return numerators, jnp.sum(numerators, axis=-1, keepdims=True)

    def head_at(kv, h):
        return pl.ds(pl.multiple_of((kv * group + h) * HEAD_DIM, HEAD_DIM), HEAD_DIM)

    def keys_and_values(qkv, kv):
        keys = turn(qkv[:, pl.ds(gq + kv * HEAD_DIM, HEAD_DIM)], 1.0).astype(SLIM)
        return keys, qkv[:, pl.ds(gq + kvw + kv * HEAD_DIM, HEAD_DIM)].astype(SLIM)

    for kv in range(kvw // HEAD_DIM):
        keys, values = keys_and_values(qkv_f, kv)

        @pl.loop(0, group)
        def _(h):
            at = head_at(kv, h)
            numerators, totals = weigh(turn(qkv_f[:, at], 1.0).astype(SLIM), keys)
            result = dot(numerators.astype(SLIM), values, ((1,), (0,))) / totals
            mixed[:, :, at] = result.astype(SLIM).reshape(n, rows, HEAD_DIM)

    to_all(mixed_copies, begin)

    from_all(small_copies)
    for kv in range(kvw // HEAD_DIM):
        keys, values = keys_and_values(qkv_b, kv)

        def head(h, sums):
            at = head_at(kv, h)
            queries = turn(qkv_b[:, at], 1.0).astype(SLIM)
            numerators, totals = weigh(queries, keys)
            rounded = numerators.astype(SLIM)
            summed = dot(rounded, values, ((1,), (0,)))
            summed_grad = mg[:, :, at].reshape(n * rows, HEAD_DIM).astype(WIDE) / totals
            totals_grad = -jnp.sum(summed_grad * (summed / totals), axis=-1, keepdims=True)
            narrow_grad = summed_grad.astype(SLIM)
            numer_grad = dot(narrow_grad, values, ((1,), (1,))) + totals_grad
            score_grad = (numerators * numer_grad * scale).astype(SLIM)
            query_grad = dot(score_grad, keys, ((1,), (0,))).astype(SLIM)
            dqkv[:, at] = turn(query_grad.astype(WIDE), -1.0).astype(SLIM)
            key_grad, value_grad = sums
            return (
                key_grad + dot(score_grad, queries, ((0,), (0,))),
                value_grad + dot(rounded, narrow_grad, ((0,), (0,))),
            )

        nothing = jnp.zeros(keys.shape, WIDE)
        key_grad, value_grad = lax.fori_loop(0, group, head, (nothing, nothing))
        dqkv[:, pl.ds(gq + kv * HEAD_DIM, HEAD_DIM)] = turn(
            key_grad.astype(SLIM).astype(WIDE), -1.0
        ).astype(SLIM)
        dqkv[:, pl.ds(gq + kvw + kv * HEAD_DIM, HEAD_DIM)] = value_grad.astype(SLIM)

    def sum_copy(side, r, block, target):
        return remote(
            part.at[block], inbox.at[side, r - 1], bsend.at[side, r], brecv.at[side, r - 1], (section, target)
        )

    def partial_grad(block, sides_in, r):
        mine_rows = dqkv[pl.ds(pl.multiple_of(block * rows, 16), rows), :]
        for j in range(n):
            part[block, :, pl.ds(j * depth, depth)] = lax.dot_general(
                mine_rows, wh[j], (((1,), (1,)), ((), ())), preferred_element_type=WIDE
            ).astype(SLIM)
        for side in sides_in:
            _, there = behind(side, 1)

            @pl.when(there)
            def _():
                sum_copy(side, r + 1, block, me).wait_recv()
                part[block] = (part[block].astype(WIDE) + inbox[side, r].astype(WIDE)).astype(SLIM)

    def sum_step(r):
        for side in (0, 1):
            block, there = peer(side, r)
            target, _ = peer(side, 1)

            @pl.when(there)
            def _():
                partial_grad(block, (side,), r)
                sum_copy(side, r, block, target).start()

    sum_step(n - 1)
    total = tokens[...].astype(WIDE)
    total += jnp.dot(
        mixed[me], wo[pl.ds(pl.multiple_of(me * gq, 128), gq), :], preferred_element_type=WIDE
    )
    from_all(mixed_copies)
    for k in range(1, n):
        source = lax.rem(me + k, n)
        at = pl.ds(pl.multiple_of(source * gq, 128), gq)
        total += jnp.dot(mixed_in[source], wo[at, :], preferred_element_type=WIDE)
    produced[...] = total.astype(SLIM)
    ahead_copy = remote(produced, ahead, csend.at[0], crecv.at[0], (following, me))
    ahead_copy.start()
    for r in range(n - 2, 0, -1):
        sum_step(r)
    partial_grad(me, (0, 1), 0)

    widened = saved[...].astype(WIDE)
    inverse = lax.rsqrt(jnp.mean(widened * widened, axis=-1, keepdims=True) + norm_eps)
    scaled = part[me].astype(WIDE) * gain[...]
    inner = jnp.mean(scaled * widened, axis=-1, keepdims=True)
    project_grad = inverse * scaled - widened * (inverse * inverse * inverse * inner)
    grads[...] = up[...] + project_grad.astype(SLIM)
    back_copy = remote(grads, back, csend.at[1], crecv.at[1], (preceding, me))
    back_copy.start()

    to_all(lambda side, t, target: weight_copies(side, t, target, me), leave)
    for copies in (small_copies, place_copies, mixed_copies):
        to_all(copies, leave)
    for t in range(1, n):
        for side in (0, 1):
            block, there = behind(side, t - 1)
            target, fits = peer(side, 1)

            @pl.when(jnp.logical_and(there, fits))
            def _():
                for batch in (0, 1):
                    leave(row_copies(batch, side, t, block, target))

            block, there = peer(side, t)
            pl.when(there)(lambda: leave([sum_copy(side, t, block, target)]))
    ahead_copy.wait()
    back_copy.wait()


def norm_kernel(first, second, gain, first_out, second_out):
    for tokens, normed in ((first, first_out), (second, second_out)):
        widened = tokens[...].astype(WIDE)
        inverse = lax.rsqrt(jnp.mean(widened * widened, axis=-1, keepdims=True) + norm_eps)
        normed[...] = (widened * inverse * gain[...]).astype(SLIM)


def hand_kernel(first, second, first_out, second_out):
    first_out[...] = first[...]
    second_out[...] = second[...]


def by_heads(n, sections):
    def step(
        section_inputs, saved_inputs, output_grads, token_positions, norm_gain,
        query_weight, keyval_weight, output_weight,
    ):
        _, rows, width = section_inputs.shape
        _, depth, query_width = query_weight.shape
        gq = query_width // n
        wide = gq + keyval_weight.shape[2] // n

        half_dim = HEAD_DIM // 2
        frequency = rope_base ** (-2.0 * np.arange(half_dim) / HEAD_DIM)
        signs = np.ones(half_dim)
        waves = jnp.asarray(
            np.stack([np.concatenate([frequency, frequency]), np.concatenate([-signs, signs])]), WIDE
        )

        def shaped(shape, kind=SLIM):
            return jax.ShapeDtypeStruct(shape, kind)

        def held(*shape, kind=SLIM):
            return pltpu.VMEM(shape, kind)

        pair = (shaped((rows, width)), shaped((rows, width)))
        normed_f, normed_b = pl.pallas_call(
            norm_kernel, out_shape=pair, in_specs=[VMEM] * 3, out_specs=(VMEM,) * 2, name="norm"
        )(section_inputs[0], saved_inputs[0], norm_gain)
        dma = pltpu.SemaphoreType.DMA
        ahead, back = pl.pallas_call(
            functools.partial(layer_kernel, n, sections),
            out_shape=pair,
            in_specs=[VMEM, VMEM, VMEM, ANY, ANY, ANY, VMEM, VMEM, VMEM, VMEM, VMEM],
            out_specs=(VMEM,) * 2,
            scratch_shapes=[
                held(n, rows, width), held(n, rows, width),
                held(n, rows, gq), held(n, rows, gq), held(query_width, width), held(n, depth, wide),
                held(n, 1, rows, kind=jnp.int32), held(n, rows, HEAD_DIM, kind=WIDE),
                held(n * rows, HEAD_DIM, kind=WIDE), held(n * rows, HEAD_DIM, kind=WIDE),
                held(n * rows, wide, kind=WIDE), held(n * rows, wide, kind=WIDE),
                held(n, rows, gq), held(n * rows, wide), held(n, rows, gq),
                held(n, rows, width), held(2, n, rows, width),
                held(rows, width), held(rows, width),
                *[dma((2, n))] * 4, *[dma((2, n, 3))] * 2, *[dma((2, n))] * 8, *[dma((2,))] * 2, dma((4,)),
            ],
            compiler_params=pltpu.CompilerParams(
                collective_id=0, has_side_effects=True, vmem_limit_bytes=60 * 2**20
            ),
            name="layer",
        )(
            normed_f, normed_b, output_grads[0], output_weight[0],
            query_weight[0], keyval_weight[0], token_positions[None], waves,
            section_inputs[0], saved_inputs[0], norm_gain,
        )
        ahead, back = pl.pallas_call(
            hand_kernel, out_shape=pair, in_specs=[VMEM] * 2, out_specs=(VMEM,) * 2, name="hand"
        )(ahead, back)
        return (ahead[None], back[None])

    return step


def solution(mesh):
    placed = (
        P("section", "ctx", None),
        P("section", "ctx", None),
        P("section", "ctx", None),
        P("ctx"),
        P("section", None),
        P("section", "ctx", None),
        P("section", "ctx", None),
        P("section", None, None),
    )
    n, sections = mesh.shape["ctx"], mesh.shape["section"]

    def chosen(*blocks):
        kv_heads = blocks[6].shape[2] // (2 * HEAD_DIM)
        if n > 1 and sections > 2 and kv_heads % n == 0:
            return by_heads(n, sections)(*blocks)
        return shards(*blocks)

    return jax.shard_map(
        chosen,
        mesh=mesh,
        in_specs=placed,
        out_specs=(P("section", "ctx", None), P("section", "ctx", None)),
        check_vma=False,
    )
```

profile of v0, /device:TPU:0, one launch (start us, length us, event | category | flops | bytes accessed | tf_op | source)
XLA Modules:
  0.0 192.7 jit_solution(16477860874310066967)
XLA Ops:
  0.6 2.4 %norm.1 = (bf16[112,2048]{1,0:T(8,128)(2,1)}, bf16[112,2048]{1,0:T(8,128)(2,1)}) custom-call(bf16[112,2048]{1,0:T(8,128)(2,1)} %bitcast.11, bf16[112,2048]{1,0:T(8,128)(2,1)} %bitcast.13, f32[1,2048]{1,0:T(1,128)} %gain.3), custom_call_target="tpu_custom_call" | custom-call | tf_op jit(solution)/shard_map/norm/pallas_call | solution.py:521
  3.0 187.7 %layer.1 = (bf16[112,2048]{1,0:T(8,128)(2,1)}, bf16[112,2048]{1,0:T(8,128)(2,1)}) custom-call(bf16[112,2048]{1,0:T(8,128)(2,1)} %get-tuple-element.8.nf, bf16[112,2048]{1,0:T(8,128)(2,1)} %get-tuple-element.9.nb, bf16[112,2048]{1,0:T(8,128)(2,1)} %bitcast.16, bf16[2048,2048]{1,0:T(8,128)(2,1)} %bitcast.9, bf16[512,2048]{1,0:T(8,128)(2,1)} %bitcast.10, ...), custom_call_target="tpu_custom_call" | custom-call | tf_op jit(solution)/shard_map/layer/pallas_call | solution.py:525
  190.6 2.1 %hand.1 = (bf16[112,2048]{1,0:T(8,128)(2,1)}, bf16[112,2048]{1,0:T(8,128)(2,1)}) custom-call(bf16[112,2048]{1,0:T(8,128)(2,1)} %get-tuple-element.10.first, bf16[112,2048]{1,0:T(8,128)(2,1)} %get-tuple-element.11.second), custom_call_target="tpu_custom_call" | custom-call | tf_op jit(solution)/shard_map/hand/pallas_call | solution.py:550
where the time goes:
time: 195 us; the launch traced here: 193 us
  Pallas kernels  192 us (98%)
    pallas_call x1, Pallas kernels, step(): pl.pallas_call(functools.partial(layer_kernel, n, sections), out_shape=pa...  188 us

commit v1 on v0

v1 whole, which is shorter than its diff:
```python
import functools

import jax
import jax.numpy as jnp
import numpy as np
from jax import lax
from jax.experimental import pallas as pl
from jax.experimental.pallas import tpu as pltpu
from jax.sharding import PartitionSpec as P

HEAD_DIM = 128


norm_eps = 1e-05
rope_base = 500000.0


def from_behind(block, axis, distance):
    devices = range(lax.axis_size(axis))
    route = [((i - distance) % len(devices), i) for i in devices]
    return lax.ppermute(block, axis, route)


def rotate(matrix, positions):
    half_dim = matrix.shape[-1] // 2
    frequency = rope_base ** (-2.0 * jnp.arange(half_dim, dtype=jnp.float32) / matrix.shape[-1])
    angles = positions.astype(jnp.float32)[:, None] * frequency[None, :]
    cos_table = jnp.cos(angles)[:, None, :]
    sin_table = jnp.sin(angles)[:, None, :]
    leading = matrix[..., :half_dim]
    trailing = matrix[..., half_dim:]
    return jnp.concatenate(
        [leading * cos_table - trailing * sin_table, trailing * cos_table + leading * sin_table],
        axis=-1,
    )


def project(tokens, gain, query_matrix, keyval_matrix, positions):
    widened = tokens.astype(jnp.float32)
    inverse = lax.rsqrt(jnp.mean(widened * widened, axis=-1, keepdims=True) + norm_eps)
    normed = (widened * inverse * gain[None, :]).astype(jnp.bfloat16)
    row_count = tokens.shape[0]
    query_full = jnp.dot(normed, query_matrix, preferred_element_type=jnp.float32)
    keyval_full = jnp.dot(normed, keyval_matrix, preferred_element_type=jnp.float32)
    queries = rotate(query_full.reshape(row_count, -1, HEAD_DIM), positions).astype(jnp.bfloat16)
    paired = keyval_full.reshape(row_count, 2, -1, HEAD_DIM)
    key_rows = rotate(paired[:, 0], positions).astype(jnp.bfloat16)
    value_rows = paired[:, 1].astype(jnp.bfloat16)
    return (queries, key_rows, value_rows)


def attend(queries, key_wide, value_wide, query_pos, key_pos, narrow):
    row_count = queries.shape[0]
    kv_count = key_wide.shape[1]
    head_size = queries.shape[2]
    group_size = queries.shape[1] // kv_count
    grouped = jnp.moveaxis(queries.reshape(row_count, kv_count, group_size, head_size), 1, 0)
    key_heads = jnp.moveaxis(key_wide, 1, 0)
    value_heads = jnp.moveaxis(value_wide, 1, 0)
    visible = (key_pos[None, :] <= query_pos[:, None])[None]

    def one_head(block):
        query_block, key_block, value_block = block
        scores = jnp.einsum(
            "rgd,sd->grs", query_block, key_block, preferred_element_type=jnp.float32
        ) * head_size ** (-0.5)
        masked = jnp.where(visible, scores, -1e30)
        row_max = lax.stop_gradient(jnp.max(masked, axis=-1, keepdims=True))
        numerators = jnp.where(visible, jnp.exp(masked - row_max), 0.0)
        totals = jnp.sum(numerators, axis=-1)
        if narrow:
            rounded = numerators.astype(jnp.bfloat16)
        else:
            rounded = lax.optimization_barrier(numerators.astype(jnp.bfloat16)).astype(jnp.float32)
        summed = jnp.einsum("grs,sd->rgd", rounded, value_block, preferred_element_type=jnp.float32)
        return summed / jnp.transpose(totals, (1, 0))[..., None]

    averaged = lax.map(one_head, (grouped, key_heads, value_heads))
    return jnp.moveaxis(averaged, 0, 1).reshape(row_count, -1).astype(jnp.bfloat16)


def finish(tokens, mixed, output_matrix):
    return (
        tokens.astype(jnp.float32)
        + jnp.dot(mixed, output_matrix, preferred_element_type=jnp.float32)
    ).astype(jnp.bfloat16)


def shards(
    section_inputs,
    saved_inputs,
    output_grads,
    token_positions,
    norm_gain,
    query_weight,
    keyval_weight,
    output_weight,
):
    key_positions = lax.all_gather(token_positions, "ctx", axis=0, tiled=True)
    full_query, full_keyval = (
        lax.all_gather(query_weight[0], "ctx", axis=0, tiled=True),
        lax.all_gather(keyval_weight[0], "ctx", axis=0, tiled=True),
    )
    full_output = output_weight[0]
    gain = norm_gain[0]
    forward_tokens = section_inputs[0]
    saved_tokens = saved_inputs[0]
    upstream = output_grads[0]

    def projector(tokens):
        return project(tokens, gain, full_query, full_keyval, token_positions)

    def attention_wide(queries, key_wide, value_wide):
        return attend(queries, key_wide, value_wide, token_positions, key_positions, False)

    def finishing(tokens, mixed):
        return finish(tokens, mixed, full_output)

    forward_queries, forward_keys, forward_values = projector(forward_tokens)
    (backward_queries, backward_keys, backward_values), back_project = jax.vjp(
        projector, saved_tokens
    )
    forward_keyset, forward_valueset = (
        lax.all_gather(forward_keys, "ctx", axis=0, tiled=True),
        lax.all_gather(forward_values, "ctx", axis=0, tiled=True),
    )
    mixed = attend(
        forward_queries, forward_keyset, forward_valueset, token_positions, key_positions, True
    )
    produced = finishing(forward_tokens, mixed)
    sent_on = from_behind(produced[None], "section", 1)
    backward_keyset, backward_valueset = (
        lax.all_gather(backward_keys, "ctx", axis=0, tiled=True),
        lax.all_gather(backward_values, "ctx", axis=0, tiled=True),
    )
    mixed, back_attend = jax.vjp(
        attention_wide,
        backward_queries.astype(jnp.float32),
        backward_keyset.astype(jnp.float32),
        backward_valueset.astype(jnp.float32),
    )
    produced, back_finish = jax.vjp(finishing, saved_tokens, mixed)
    residual_grad, mixed_grad = back_finish(upstream)
    query_grad, key_partial, value_partial = back_attend(mixed_grad)
    key_grads = lax.psum_scatter(
        key_partial.astype(jnp.bfloat16), "ctx", scatter_dimension=0, tiled=True
    )
    value_grads = lax.psum_scatter(
        value_partial.astype(jnp.bfloat16), "ctx", scatter_dimension=0, tiled=True
    )
    (project_grad,) = back_project((query_grad.astype(jnp.bfloat16), key_grads, value_grads))
    sent_back = from_behind((residual_grad + project_grad)[None], "section", -1)
    return (sent_on, sent_back)


MESH = pl.DeviceIdType.MESH
VMEM = pl.BlockSpec(memory_space=pltpu.VMEM)
ANY = pl.BlockSpec(memory_space=pl.ANY)
WIDE = jnp.float32
SLIM = jnp.bfloat16


def remote(src, dst, send, recv, device):
    return pltpu.make_async_remote_copy(
        src_ref=src, dst_ref=dst, send_sem=send, recv_sem=recv, device_id=device, device_id_type=MESH
    )


def layer_kernel(
    n, sections, tokens, saved, up, gain, wo_hbm, wq, wkv, pos, waves, ahead, back,
    nx, mine, mgl, mg, wo, wh, posg, bias, cos, sin, keys, values, dkey, dval, mixed, mixed_in, dqkv,
    part, from_mate, from_z, dn, produced, grads,
    nsend, nrecv, wsend, wrecv, msend, mrecv, psend, precv, asend, arecv, bsend, brecv, zsend, zrecv,
    osend, orecv, csend, crecv, own,
):
    section = lax.axis_index("section")
    me = lax.axis_index("ctx")
    half = n // 2
    core = lax.rem(section, 2)
    base = section - core
    mate = base + 1 - core
    side = me // half
    served = base + side
    lead = core == side
    partner = 2 * side * half + half - 1 - me
    edge = half - 1 + side
    at_edge = me == edge
    group_at = lax.rem(me, half) * 2 + core
    near, far = half - side, (n - 1) * (1 - side)
    depth, _ = wq.shape
    rows, width = tokens.shape
    gq = mg.shape[2]
    group = gq // HEAD_DIM
    kv_half = wkv.shape[1] // 2
    total_rows = n * rows
    scale = HEAD_DIM ** (-0.5)
    following, preceding = lax.rem(section + 1, sections), lax.rem(section + sections - 1, sections)
    pieces = group + 2

    barrier = pltpu.get_barrier_semaphore()
    for k in range(1, n):
        for other in (section, mate):
            pl.semaphore_signal(barrier, inc=1, device_id=(other, lax.rem(me + k, n)), device_id_type=MESH)
    for other in (mate, following, preceding):
        pl.semaphore_signal(barrier, inc=1, device_id=(other, me), device_id_type=MESH)

    wo_copy = pltpu.make_async_copy(wo_hbm, wo, own.at[0])
    wo_copy.start()

    def normed(block):
        widened = block[...].astype(WIDE)
        inverse = lax.rsqrt(jnp.mean(widened * widened, axis=-1, keepdims=True) + norm_eps)
        return (widened * inverse * gain[...]).astype(SLIM)

    for batch, block in enumerate((tokens, saved)):
        mine[batch] = normed(block)

    @pl.when(lead)
    def _():
        for batch in (0, 1):
            nx[batch, me] = mine[batch]

    posg[me] = pos[...]
    pl.semaphore_wait(barrier, 2 * n + 1)

    def seat(owner_core, j):
        return (base + j % 2, owner_core * half + j // 2)

    def token_copy(batch, lane, src, block, device):
        return remote(src, nx.at[batch, block], nsend.at[batch, lane, block], nrecv.at[batch, block], device)

    def to_mate(batch, block):
        return token_copy(batch, 0, nx.at[batch, block], block, (mate, me))

    def to_partner(batch, block):
        return token_copy(batch, 1, nx.at[batch, block], block, (section, partner))

    def to_edge(batch):
        return token_copy(batch, 0, mine.at[batch], me, (section, half - 1 + core))

    def piece_source(j, piece):
        if piece < group:
            return wq.at[:, pl.ds(j * gq + piece * HEAD_DIM, HEAD_DIM)], piece * HEAD_DIM
        value = piece - group
        return wkv.at[:, pl.ds(value * kv_half + j * HEAD_DIM, HEAD_DIM)], piece * HEAD_DIM

    def weight_copy(j, piece):
        src, to = piece_source(j, piece)
        return remote(
            src, wh.at[me, :, pl.ds(to, HEAD_DIM)], wsend.at[j, piece], wrecv.at[me, piece], seat(core, j)
        )

    def weight_here(j, piece):
        src, to = piece_source(j, piece)
        return pltpu.make_async_copy(src, wh.at[me, :, pl.ds(to, HEAD_DIM)], wrecv.at[me, piece])

    def weight_arrived(block, piece):
        dst = wh.at[block, :, pl.ds(piece * HEAD_DIM, HEAD_DIM)]
        remote(dst, dst, wsend.at[0, 0], wrecv.at[block, piece], (section, me)).wait_recv()

    def here(j):
        return jnp.logical_and(lead, group_at == j)

    def send_weights(piece):
        for j in range(n):
            pl.when(here(j))(lambda: weight_here(j, piece).start())
            pl.when(jnp.logical_not(here(j)))(lambda: weight_copy(j, piece).start())

    def grad_copy(j):
        return remote(mgl.at[j], mg.at[me], msend.at[j], mrecv.at[me], seat(core, j))

    def place_copy(k):
        return remote(pos, posg.at[me], psend.at[k], precv.at[me], (section, lax.rem(me + k, n)))

    @pl.when(lead)
    def _():
        for batch in (0, 1):
            to_partner(batch, me).start()
        for batch in (0, 1):
            to_mate(batch, me).start()

    @pl.when(jnp.logical_not(lead))
    def _():
        for batch in (0, 1):
            to_edge(batch).start()

    for k in range(1, n):
        place_copy(k).start()
    send_weights(group)
    send_weights(group + 1)

    wo_copy.wait()
    for j in range(n):
        mgl[j] = lax.dot_general(
            up[...], wo[pl.ds(j * gq, gq), :], (((1,), (1,)), ((), ())), preferred_element_type=WIDE
        ).astype(SLIM)
    for j in range(n):
        @pl.when(here(j))
        def _():
            mg[me] = mgl[j]

        pl.when(jnp.logical_not(here(j)))(lambda: grad_copy(j).start())

    @pl.when(jnp.logical_not(lead))
    def _():
        for piece in range(group):
            send_weights(piece)

    def token_arrived(batch, block):
        dst = nx.at[batch, block]
        remote(dst, dst, nsend.at[0, 0, 0], nrecv.at[batch, block], (section, me)).wait_recv()

    @pl.when(lead)
    def _():
        for batch in (0, 1):
            for block, outer in ((partner, False), (near, True), (far, True)):
                token_arrived(batch, block)
                if outer:
                    pl.when(at_edge)(lambda: to_partner(batch, block).start())
                to_mate(batch, block).start()
        for piece in range(group):
            send_weights(piece)

    for k in range(1, n):
        source = lax.rem(me + k, n)
        remote(pos, posg.at[source], psend.at[0], precv.at[source], (section, me)).wait_recv()
    columns = []
    for j in range(n):
        column = jnp.transpose(jnp.broadcast_to(posg[j].astype(WIDE), (HEAD_DIM, rows)))
        angles = column * waves[0:1, :]
        at = pl.ds(j * rows, rows)
        cos[at, :] = jnp.cos(angles)
        sin[at, :] = jnp.sin(angles) * waves[1:2, :]
        columns.append(column)
    column = jnp.concatenate(columns, axis=0)
    bias[...] = jnp.where(jnp.transpose(column)[0:1, :] <= column[:, 0:1], 0.0, -1e30)

    @pl.when(jnp.logical_not(lead))
    def _():
        for batch in (0, 1):
            for block in range(n):
                token_arrived(batch, block)

    def turn(block, sign):
        return block * cos[...] + sign * (pltpu.roll(block, HEAD_DIM // 2, 1) * sin[...])

    def dot(a, b, dims):
        return lax.dot_general(a, b, (dims, ((), ())), preferred_element_type=WIDE)

    def projected(batch, at):
        result = None
        for j in range(n):
            term = dot(
                nx[batch, :, :, pl.ds(j * depth, depth)].reshape(total_rows, depth), wh[j, :, at], ((1,), (0,))
            )
            result = term if result is None else result + term
        return result

    for piece in (group, group + 1):
        for j in range(n):
            weight_arrived(j, piece)
    for batch in (0, 1):
        both = projected(batch, pl.ds(gq, 2 * HEAD_DIM))
        keys[batch] = turn(both[:, :HEAD_DIM], 1.0).astype(SLIM)
        values[batch] = both[:, HEAD_DIM:].astype(SLIM)

    def weigh(queries, key_block):
        masked = dot(queries, key_block, ((1,), (1,))) * scale + bias[...]
        numerators = jnp.exp(masked - jnp.max(masked, axis=-1, keepdims=True))
        return numerators, jnp.sum(numerators, axis=-1, keepdims=True)

    def mixed_copy(block, h):
        return remote(
            mixed.at[block, h], mixed_in.at[group_at, h], asend.at[block, h], arecv.at[group_at, h], (served, block)
        )

    def elsewhere(block):
        return jnp.logical_not(jnp.logical_and(lead, me == block))

    dkey[...] = jnp.zeros_like(dkey)
    dval[...] = jnp.zeros_like(dval)

    for h in range(group):
        at = pl.ds(h * HEAD_DIM, HEAD_DIM)
        for j in range(n):
            weight_arrived(j, h)
        queries = turn(projected(0, at), 1.0).astype(SLIM)
        numerators, totals = weigh(queries, keys[0])
        result = dot(numerators.astype(SLIM), values[0], ((1,), (0,))) / totals
        mixed[:, h] = result.astype(SLIM).reshape(n, rows, HEAD_DIM)

        for block in range(n):
            pl.when(elsewhere(block))(lambda: mixed_copy(block, h).start())

        @pl.when(lead)
        def _():
            mixed_in[group_at, h] = mixed[me, h]

        if h == 0:
            for block in range(n):
                pl.when(elsewhere(block))(
                    lambda: remote(
                        mg.at[block], mg.at[block], msend.at[0], mrecv.at[block], (section, me)
                    ).wait_recv()
                )
        queries = turn(projected(1, at), 1.0).astype(SLIM)
        numerators, totals = weigh(queries, keys[1])
        rounded = numerators.astype(SLIM)
        summed = dot(rounded, values[1], ((1,), (0,)))
        summed_grad = mg[:, :, at].reshape(total_rows, HEAD_DIM).astype(WIDE) / totals
        totals_grad = -jnp.sum(summed_grad * (summed / totals), axis=-1, keepdims=True)
        narrow_grad = summed_grad.astype(SLIM)
        numer_grad = dot(narrow_grad, values[1], ((1,), (1,))) + totals_grad
        score_grad = (numerators * numer_grad * scale).astype(SLIM)
        query_grad = dot(score_grad, keys[1], ((1,), (0,))).astype(SLIM)
        dqkv[:, at] = turn(query_grad.astype(WIDE), -1.0).astype(SLIM)
        dkey[...] += dot(score_grad, queries, ((0,), (0,)))
        dval[...] += dot(rounded, narrow_grad, ((0,), (0,)))

    dqkv[:, pl.ds(gq, HEAD_DIM)] = turn(dkey[...].astype(SLIM).astype(WIDE), -1.0).astype(SLIM)
    dqkv[:, pl.ds(gq + HEAD_DIM, HEAD_DIM)] = dval[...].astype(SLIM)

    def partial_grad(block):
        block_rows = dqkv[pl.ds(pl.multiple_of(block * rows, 16), rows), :]
        for j in range(n):
            part[block, :, pl.ds(j * depth, depth)] = dot(block_rows, wh[j], ((1,), (1,))).astype(SLIM)

    def mate_sum(block):
        return remote(part.at[block], from_mate.at[block], bsend.at[block], brecv.at[block], (mate, me))

    def partner_sum(block):
        return remote(part.at[block], from_z.at[block], zsend.at[block], zrecv.at[block], (section, partner))

    def owner_sum(block):
        return remote(part.at[block], dn, osend.at[block], orecv.at[0], (section, block))

    def add_mate(block):
        mate_sum(block).wait_recv()
        part[block] = (part[block].astype(WIDE) + from_mate[block].astype(WIDE)).astype(SLIM)

    def add_partner(block):
        partner_sum(block).wait_recv()
        return (part[block].astype(WIDE) + from_z[block].astype(WIDE)).astype(SLIM)

    for block in (near, far, partner, me):
        partial_grad(block)
        pl.when(jnp.logical_not(lead))(lambda: mate_sum(block).start())

        @pl.when(lead)
        def _():
            add_mate(block)

        if block is partner:
            pl.when(lead)(lambda: partner_sum(block).start())
        elif block is not me:
            inner = jnp.logical_and(lead, jnp.logical_not(at_edge))
            pl.when(inner)(lambda: partner_sum(block).start())

    @pl.when(jnp.logical_and(lead, at_edge))
    def _():
        for block in (near, far):
            part[block] = add_partner(block)
            owner_sum(block).start()

    total = tokens[...].astype(WIDE)
    for j in range(n):
        def arrived():
            for h in range(group):
                dst = mixed_in.at[j, h]
                remote(dst, dst, asend.at[0, 0], arecv.at[j, h], (section, me)).wait_recv()

        pl.when(jnp.logical_not(here(j)))(arrived)
        for h in range(group):
            total += jnp.dot(
                mixed_in[j, h], wo[pl.ds(j * gq + h * HEAD_DIM, HEAD_DIM), :], preferred_element_type=WIDE
            )
    produced[...] = total.astype(SLIM)
    ahead_copy = remote(produced, ahead, csend.at[0], crecv.at[0], (following, me))
    ahead_copy.start()

    @pl.when(lead)
    def _():
        dn[...] = add_partner(me)

    @pl.when(jnp.logical_not(lead))
    def _():
        owner_sum(me).wait_recv()

    widened = saved[...].astype(WIDE)
    inverse = lax.rsqrt(jnp.mean(widened * widened, axis=-1, keepdims=True) + norm_eps)
    scaled = dn[...].astype(WIDE) * gain[...]
    inner_mean = jnp.mean(scaled * widened, axis=-1, keepdims=True)
    project_grad = inverse * scaled - widened * (inverse * inverse * inverse * inner_mean)
    grads[...] = up[...] + project_grad.astype(SLIM)
    back_copy = remote(grads, back, csend.at[1], crecv.at[1], (preceding, me))
    back_copy.start()

    @pl.when(lead)
    def _():
        for batch in (0, 1):
            for block in range(n):
                to_mate(batch, block).wait_send()
            to_partner(batch, me).wait_send()
            for block in (near, far):
                pl.when(at_edge)(lambda: to_partner(batch, block).wait_send())

    @pl.when(jnp.logical_not(lead))
    def _():
        for batch in (0, 1):
            to_edge(batch).wait_send()

    for k in range(1, n):
        place_copy(k).wait_send()
    for j in range(n):
        @pl.when(jnp.logical_not(here(j)))
        def _():
            for piece in range(pieces):
                weight_copy(j, piece).wait_send()
            grad_copy(j).wait_send()

        @pl.when(elsewhere(j))
        def _():
            for h in range(group):
                mixed_copy(j, h).wait_send()

    for block in range(n):
        pl.when(jnp.logical_not(lead))(lambda: mate_sum(block).wait_send())

    @pl.when(lead)
    def _():
        partner_sum(partner).wait_send()
        for block in (near, far):
            pl.when(at_edge)(lambda: owner_sum(block).wait_send())
            pl.when(jnp.logical_not(at_edge))(lambda: partner_sum(block).wait_send())

    ahead_copy.wait()
    back_copy.wait()


def hand_kernel(first, second, first_out, second_out):
    first_out[...] = first[...]
    second_out[...] = second[...]


def by_pairs(n, sections):
    def step(
        section_inputs, saved_inputs, output_grads, token_positions, norm_gain,
        query_weight, keyval_weight, output_weight,
    ):
        _, rows, width = section_inputs.shape
        _, depth, query_width = query_weight.shape
        gq = query_width // n
        group = gq // HEAD_DIM
        wide = gq + keyval_weight.shape[2] // n

        half_dim = HEAD_DIM // 2
        frequency = rope_base ** (-2.0 * np.arange(half_dim) / HEAD_DIM)
        signs = np.ones(half_dim)
        waves = jnp.asarray(
            np.stack([np.concatenate([frequency, frequency]), np.concatenate([-signs, signs])]), WIDE
        )

        def shaped(shape, kind=SLIM):
            return jax.ShapeDtypeStruct(shape, kind)

        def held(*shape, kind=SLIM):
            return pltpu.VMEM(shape, kind)

        pair = (shaped((rows, width)), shaped((rows, width)))
        dma = pltpu.SemaphoreType.DMA
        ahead, back = pl.pallas_call(
            functools.partial(layer_kernel, n, sections),
            out_shape=pair,
            in_specs=[VMEM, VMEM, VMEM, VMEM, ANY, ANY, ANY, VMEM, VMEM],
            out_specs=(VMEM,) * 2,
            scratch_shapes=[
                held(2, n, rows, width), held(2, rows, width),
                held(n, rows, gq), held(n, rows, gq), held(query_width, width), held(n, depth, wide),
                held(n, 1, rows, kind=jnp.int32), held(n * rows, n * rows, kind=WIDE),
                held(n * rows, HEAD_DIM, kind=WIDE), held(n * rows, HEAD_DIM, kind=WIDE),
                held(2, n * rows, HEAD_DIM), held(2, n * rows, HEAD_DIM),
                held(n * rows, HEAD_DIM, kind=WIDE), held(n * rows, HEAD_DIM, kind=WIDE),
                held(n, group, rows, HEAD_DIM), held(n, group, rows, HEAD_DIM), held(n * rows, wide),
                held(n, rows, width), held(n, rows, width), held(n, rows, width), held(rows, width),
                held(rows, width), held(rows, width),
                dma((2, 2, n)), dma((2, n)), dma((n, group + 2)), dma((n, group + 2)),
                *[dma((n,))] * 4, *[dma((n, group))] * 2, *[dma((n,))] * 5, dma((1,)),
                *[dma((2,))] * 2, dma((1,)),
            ],
            compiler_params=pltpu.CompilerParams(
                collective_id=0, has_side_effects=True, vmem_limit_bytes=60 * 2**20
            ),
            name="layer",
        )(
            section_inputs[0], saved_inputs[0], output_grads[0], norm_gain, output_weight[0],
            query_weight[0], keyval_weight[0], token_positions[None], waves,
        )
        ahead, back = pl.pallas_call(
            hand_kernel, out_shape=pair, in_specs=[VMEM] * 2, out_specs=(VMEM,) * 2, name="hand"
        )(ahead, back)
        return (ahead[None], back[None])

    return step


def solution(mesh):
    placed = (
        P("section", "ctx", None),
        P("section", "ctx", None),
        P("section", "ctx", None),
        P("ctx"),
        P("section", None),
        P("section", "ctx", None),
        P("section", "ctx", None),
        P("section", None, None),
    )
    n, sections = mesh.shape["ctx"], mesh.shape["section"]

    def chosen(*blocks):
        kv_heads = blocks[6].shape[2] // (2 * HEAD_DIM)
        if n == 4 and sections > 2 and sections % 2 == 0 and kv_heads == n:
            return by_pairs(n, sections)(*blocks)
        return shards(*blocks)

    return jax.shard_map(
        chosen,
        mesh=mesh,
        in_specs=placed,
        out_specs=(P("section", "ctx", None), P("section", "ctx", None)),
        check_vma=False,
    )
```

time: 195 us -> 146 us (0.75)
  Pallas kernels: 192 us -> 142 us
    pallas_call x1, Pallas kernels: 188 us -> 140 us  [step(): pl.pallas_call(functools.partial(layer_kernel, n, sections), out_shape=pa...]
    pallas_call x1 -> x0, Pallas kernels: 2.35 us -> none  [step(): pl.pallas_call(norm_kernel, out_shape=pair, in_specs=[VMEM] * 3, out_spec...]
where the time goes in v1:
time: 146 us; the launch traced here: 143 us
  Pallas kernels  142 us (97%)
    pallas_call x1, Pallas kernels, step(): pl.pallas_call(functools.partial(layer_kernel, n, sections), out_shape=pa...  140 us

profile of v1, /device:TPU:0, one launch (start us, length us, event | category | flops | bytes accessed | tf_op | source)
XLA Modules:
  0.0 142.7 jit_solution(646976818134674404)
XLA Ops:
  0.6 139.9 %layer.1 = (bf16[112,2048]{1,0:T(8,128)(2,1)}, bf16[112,2048]{1,0:T(8,128)(2,1)}) custom-call(bf16[112,2048]{1,0:T(8,128)(2,1)} %bitcast.12, bf16[112,2048]{1,0:T(8,128)(2,1)} %bitcast.13, bf16[112,2048]{1,0:T(8,128)(2,1)} %bitcast.14, f32[1,2048]{1,0:T(1,128)} %gain.1, bf16[2048,2048]{1,0:T(8,128)(2,1)} %bitcast.9, bf16[512,2048]{1,0:T(8,128)(2,1)} %bitcast.10, ...), custom_call_target="tpu_custom_call" | custom-call | tf_op jit(solution)/shard_map/layer/pallas_call | solution.py:571
  140.6 2.1 %hand.1 = (bf16[112,2048]{1,0:T(8,128)(2,1)}, bf16[112,2048]{1,0:T(8,128)(2,1)}) custom-call(bf16[112,2048]{1,0:T(8,128)(2,1)} %get-tuple-element.6.first, bf16[112,2048]{1,0:T(8,128)(2,1)} %get-tuple-element.7.second), custom_call_target="tpu_custom_call" | custom-call | tf_op jit(solution)/shard_map/hand/pallas_call | solution.py:598

commit v2 on v1

--- a/solution.py
+++ b/solution.py
@@ -166,9 +166,15 @@
     )
 
 
+def row_chunks(rows):
+    tiles = rows // 16
+    sizes = [size * 16 for size in ((tiles - 1) - (tiles - 1) // 2, (tiles - 1) // 2, 1) if size]
+    return [(sum(sizes[:i]), size) for i, size in enumerate(sizes)]
+
+
 def layer_kernel(
-    n, sections, tokens, saved, up, gain, wo_hbm, wq, wkv, pos, waves, ahead, back,
-    nx, mine, mgl, mg, wo, wh, posg, bias, cos, sin, keys, values, dkey, dval, mixed, mixed_in, dqkv,
+    n, sections, tokens_hbm, saved_hbm, up_hbm, gain_hbm, wo_hbm, wq, wkv, pos_hbm, waves_hbm, ahead, back,
+    tokens, saved, up, gain, pos, waves, nx, mine, mgl, mg, wo, wh, posg, bias, cos, sin, keys, values, dkey, dval, mixed, mixed_in, dqkv,
     part, from_mate, from_z, dn, produced, grads,
     nsend, nrecv, wsend, wrecv, msend, mrecv, psend, precv, asend, arecv, bsend, brecv, zsend, zrecv,
     osend, orecv, csend, crecv, own,
@@ -204,14 +210,25 @@
     for other in (mate, following, preceding):
         pl.semaphore_signal(barrier, inc=1, device_id=(other, me), device_id_type=MESH)
 
-    wo_copy = pltpu.make_async_copy(wo_hbm, wo, own.at[0])
-    wo_copy.start()
+    loads = [
+        pltpu.make_async_copy(src, dst, own.at[i])
+        for i, (src, dst) in enumerate(
+            (
+                (gain_hbm, gain), (tokens_hbm, tokens), (saved_hbm, saved), (pos_hbm, pos), (up_hbm, up),
+                (waves_hbm, waves), (wo_hbm, wo),
+            )
+        )
+    ]
+    for load in loads:
+        load.start()
 
     def normed(block):
         widened = block[...].astype(WIDE)
         inverse = lax.rsqrt(jnp.mean(widened * widened, axis=-1, keepdims=True) + norm_eps)
         return (widened * inverse * gain[...]).astype(SLIM)
 
+    for load in loads[:4]:
+        load.wait()
     for batch, block in enumerate((tokens, saved)):
         mine[batch] = normed(block)
 
@@ -224,7 +241,7 @@
     pl.semaphore_wait(barrier, 2 * n + 1)
 
     def seat(owner_core, j):
-        return (base + j % 2, owner_core * half + j // 2)
+        return (base + lax.rem(j, 2), owner_core * half + j // 2)
 
     def token_copy(batch, lane, src, block, device):
         return remote(src, nx.at[batch, block], nsend.at[batch, lane, block], nrecv.at[batch, block], device)
@@ -240,9 +257,10 @@
 
     def piece_source(j, piece):
         if piece < group:
-            return wq.at[:, pl.ds(j * gq + piece * HEAD_DIM, HEAD_DIM)], piece * HEAD_DIM
-        value = piece - group
-        return wkv.at[:, pl.ds(value * kv_half + j * HEAD_DIM, HEAD_DIM)], piece * HEAD_DIM
+            start = j * gq + piece * HEAD_DIM
+            return wq.at[:, pl.ds(pl.multiple_of(start, HEAD_DIM), HEAD_DIM)], piece * HEAD_DIM
+        start = (piece - group) * kv_half + j * HEAD_DIM
+        return wkv.at[:, pl.ds(pl.multiple_of(start, HEAD_DIM), HEAD_DIM)], piece * HEAD_DIM
 
     def weight_copy(j, piece):
         src, to = piece_source(j, piece)
@@ -262,7 +280,8 @@
         return jnp.logical_and(lead, group_at == j)
 
     def send_weights(piece):
-        for j in range(n):
+        for i in range(n):
+            j = lax.rem(i + core * half, n)
             pl.when(here(j))(lambda: weight_here(j, piece).start())
             pl.when(jnp.logical_not(here(j)))(lambda: weight_copy(j, piece).start())
 
@@ -289,7 +308,8 @@
     send_weights(group)
     send_weights(group + 1)
 
-    wo_copy.wait()
+    for load in loads[4:]:
+        load.wait()
     for j in range(n):
         mgl[j] = lax.dot_general(
             up[...], wo[pl.ds(j * gq, gq), :], (((1,), (1,)), ((), ())), preferred_element_type=WIDE
@@ -369,40 +389,38 @@
         numerators = jnp.exp(masked - jnp.max(masked, axis=-1, keepdims=True))
         return numerators, jnp.sum(numerators, axis=-1, keepdims=True)
 
-    def mixed_copy(block, h):
+    last = group - 1
+    spans = ((0, last * HEAD_DIM), (last * HEAD_DIM, HEAD_DIM))
+
+    def mixed_copy(block, i):
+        at = pl.ds(*spans[i])
         return remote(
-            mixed.at[block, h], mixed_in.at[group_at, h], asend.at[block, h], arecv.at[group_at, h], (served, block)
+            mixed.at[block, :, at], mixed_in.at[group_at, :, at],
+            asend.at[block, i], arecv.at[group_at, i], (served, block),
         )
 
     def elsewhere(block):
         return jnp.logical_not(jnp.logical_and(lead, me == block))
 
-    dkey[...] = jnp.zeros_like(dkey)
-    dval[...] = jnp.zeros_like(dval)
-
-    for h in range(group):
+    def send_mixed(i, *blocks):
+        for block in blocks:
+            pl.when(elsewhere(block))(lambda: mixed_copy(block, i).start())
+
+    def keep_mixed(i):
+        @pl.when(lead)
+        def _():
+            at = pl.ds(*spans[i])
+            mixed_in[group_at, :, at] = mixed[me, :, at]
+
+    def forward_head(h):
         at = pl.ds(h * HEAD_DIM, HEAD_DIM)
-        for j in range(n):
-            weight_arrived(j, h)
         queries = turn(projected(0, at), 1.0).astype(SLIM)
         numerators, totals = weigh(queries, keys[0])
         result = dot(numerators.astype(SLIM), values[0], ((1,), (0,))) / totals
-        mixed[:, h] = result.astype(SLIM).reshape(n, rows, HEAD_DIM)
-
-        for block in range(n):
-            pl.when(elsewhere(block))(lambda: mixed_copy(block, h).start())
-
-        @pl.when(lead)
-        def _():
-            mixed_in[group_at, h] = mixed[me, h]
-
-        if h == 0:
-            for block in range(n):
-                pl.when(elsewhere(block))(
-                    lambda: remote(
-                        mg.at[block], mg.at[block], msend.at[0], mrecv.at[block], (section, me)
-                    ).wait_recv()
-                )
+        mixed[:, :, at] = result.astype(SLIM).reshape(n, rows, HEAD_DIM)
+
+    def backward_head(h):
+        at = pl.ds(h * HEAD_DIM, HEAD_DIM)
         queries = turn(projected(1, at), 1.0).astype(SLIM)
         numerators, totals = weigh(queries, keys[1])
         rounded = numerators.astype(SLIM)
@@ -417,83 +435,159 @@
         dkey[...] += dot(score_grad, queries, ((0,), (0,)))
         dval[...] += dot(rounded, narrow_grad, ((0,), (0,)))
 
+    dkey[...] = jnp.zeros_like(dkey)
+    dval[...] = jnp.zeros_like(dval)
+
+    for h in range(group):
+        for j in range(n):
+            weight_arrived(j, h)
+        if h == last:
+            send_mixed(0, far, near)
+        if h == 0:
+            for block in range(n):
+                pl.when(elsewhere(block))(
+                    lambda: remote(
+                        mg.at[block], mg.at[block], msend.at[0], mrecv.at[block], (section, me)
+                    ).wait_recv()
+                )
+        backward_head(h)
+        if h < last:
+            forward_head(h)
+        if h == last - 1:
+            send_mixed(0, partner, me)
+            keep_mixed(0)
+
     dqkv[:, pl.ds(gq, HEAD_DIM)] = turn(dkey[...].astype(SLIM).astype(WIDE), -1.0).astype(SLIM)
     dqkv[:, pl.ds(gq + HEAD_DIM, HEAD_DIM)] = dval[...].astype(SLIM)
 
-    def partial_grad(block):
-        block_rows = dqkv[pl.ds(pl.multiple_of(block * rows, 16), rows), :]
+    def partial_grads(first):
+        block_rows = dqkv[pl.ds(pl.multiple_of(first * rows, 16), half * rows), :]
         for j in range(n):
-            part[block, :, pl.ds(j * depth, depth)] = dot(block_rows, wh[j], ((1,), (1,))).astype(SLIM)
-
-    def mate_sum(block):
-        return remote(part.at[block], from_mate.at[block], bsend.at[block], brecv.at[block], (mate, me))
-
-    def partner_sum(block):
-        return remote(part.at[block], from_z.at[block], zsend.at[block], zrecv.at[block], (section, partner))
-
-    def owner_sum(block):
-        return remote(part.at[block], dn, osend.at[block], orecv.at[0], (section, block))
-
-    def add_mate(block):
-        mate_sum(block).wait_recv()
-        part[block] = (part[block].astype(WIDE) + from_mate[block].astype(WIDE)).astype(SLIM)
-
-    def add_partner(block):
-        partner_sum(block).wait_recv()
-        return (part[block].astype(WIDE) + from_z[block].astype(WIDE)).astype(SLIM)
-
-    for block in (near, far, partner, me):
-        partial_grad(block)
-        pl.when(jnp.logical_not(lead))(lambda: mate_sum(block).start())
-
-        @pl.when(lead)
-        def _():
-            add_mate(block)
-
-        if block is partner:
-            pl.when(lead)(lambda: partner_sum(block).start())
-        elif block is not me:
-            inner = jnp.logical_and(lead, jnp.logical_not(at_edge))
-            pl.when(inner)(lambda: partner_sum(block).start())
-
-    @pl.when(jnp.logical_and(lead, at_edge))
-    def _():
-        for block in (near, far):
-            part[block] = add_partner(block)
-            owner_sum(block).start()
+            part[pl.ds(first, half), :, pl.ds(j * depth, depth)] = (
+                dot(block_rows, wh[j], ((1,), (1,))).astype(SLIM).reshape(half, rows, depth)
+            )
+
+    chunks = row_chunks(rows)
+
+    def mate_sum(block, c):
+        at = pl.ds(*chunks[c])
+        return remote(
+            part.at[block, at], from_mate.at[block, at], bsend.at[block, c], brecv.at[block, c], (mate, me)
+        )
+
+    def partner_sum(block, c):
+        at = pl.ds(*chunks[c])
+        return remote(
+            part.at[block, at], from_z.at[block, at], zsend.at[block, c], zrecv.at[block, c], (section, partner)
+        )
+
+    def owner_sum(block, c):
+        at = pl.ds(*chunks[c])
+        return remote(part.at[block, at], dn.at[at], osend.at[block, c], orecv.at[c], (section, block))
+
+    def each_chunk(*blocks):
+        return [(block, c) for block in blocks for c in range(len(chunks))]
+
+    def summed_part(block, c, *others):
+        at = pl.ds(*chunks[c])
+        value = part[block, at].astype(WIDE)
+        for other in others:
+            value += other[block, at].astype(WIDE)
+        return value.astype(SLIM)
+
+    trailing = jnp.logical_not(lead)
+    at_lead_edge = jnp.logical_and(lead, at_edge)
+    at_lead_inner = jnp.logical_and(lead, jnp.logical_not(at_edge))
+
+    partial_grads((1 - side) * half)
+
+    @pl.when(trailing)
+    def _():
+        for block, c in each_chunk(near, far):
+            mate_sum(block, c).start()
+
+    partial_grads(side * half)
+
+    @pl.when(trailing)
+    def _():
+        for block, c in each_chunk(partner, me):
+            mate_sum(block, c).start()
+
+    def pass_on(block, c):
+        mate_sum(block, c).wait_recv()
+        part[block, pl.ds(*chunks[c])] = summed_part(block, c, from_mate)
+        partner_sum(block, c).start()
+
+    @pl.when(at_lead_inner)
+    def _():
+        for block, c in each_chunk(near):
+            pass_on(block, c)
+
+    forward_head(last)
+    send_mixed(1, far, near, partner, me)
+    keep_mixed(1)
+
+    @pl.when(at_lead_inner)
+    def _():
+        for block, c in each_chunk(far, partner):
+            pass_on(block, c)
+
+    @pl.when(at_lead_edge)
+    def _():
+        for block, c in each_chunk(partner):
+            pass_on(block, c)
+
+
+    def finish_block(block):
+        for c in range(len(chunks)):
+            mate_sum(block, c).wait_recv()
+            partner_sum(block, c).wait_recv()
+            part[block, pl.ds(*chunks[c])] = summed_part(block, c, from_mate, from_z)
+            owner_sum(block, c).start()
+
+    pl.when(at_lead_edge)(lambda: finish_block(near))
+
+    def back_copy(c):
+        at = pl.ds(*chunks[c])
+        return remote(grads.at[at], back.at[at], csend.at[c], crecv.at[c], (preceding, me))
+
+    def give_back():
+        for c, chunk in enumerate(chunks):
+            at = pl.ds(*chunk)
+
+            @pl.when(lead)
+            def _():
+                mate_sum(me, c).wait_recv()
+                partner_sum(me, c).wait_recv()
+                dn[at] = summed_part(me, c, from_mate, from_z)
+
+            pl.when(trailing)(lambda: owner_sum(me, c).wait_recv())
+            widened = saved[at].astype(WIDE)
+            inverse = lax.rsqrt(jnp.mean(widened * widened, axis=-1, keepdims=True) + norm_eps)
+            scaled = dn[at].astype(WIDE) * gain[...]
+            inner_mean = jnp.mean(scaled * widened, axis=-1, keepdims=True)
+            project_grad = inverse * scaled - widened * (inverse * inverse * inverse * inner_mean)
+            grads[at] = up[at] + project_grad.astype(SLIM)
+            back_copy(c).start()
+
+    early = jnp.logical_and(at_lead_inner, core == 0)
+    pl.when(early)(give_back)
 
     total = tokens[...].astype(WIDE)
     for j in range(n):
         def arrived():
-            for h in range(group):
-                dst = mixed_in.at[j, h]
-                remote(dst, dst, asend.at[0, 0], arecv.at[j, h], (section, me)).wait_recv()
+            for i, span in enumerate(spans):
+                dst = mixed_in.at[j, :, pl.ds(*span)]
+                remote(dst, dst, asend.at[0, 0], arecv.at[j, i], (section, me)).wait_recv()
 
         pl.when(jnp.logical_not(here(j)))(arrived)
-        for h in range(group):
-            total += jnp.dot(
-                mixed_in[j, h], wo[pl.ds(j * gq + h * HEAD_DIM, HEAD_DIM), :], preferred_element_type=WIDE
-            )
+        total += jnp.dot(mixed_in[j], wo[pl.ds(j * gq, gq), :], preferred_element_type=WIDE)
     produced[...] = total.astype(SLIM)
-    ahead_copy = remote(produced, ahead, csend.at[0], crecv.at[0], (following, me))
+    ahead_copy = remote(produced, ahead, csend.at[len(chunks)], crecv.at[len(chunks)], (following, me))
     ahead_copy.start()
-
-    @pl.when(lead)
-    def _():
-        dn[...] = add_partner(me)
-
-    @pl.when(jnp.logical_not(lead))
-    def _():
-        owner_sum(me).wait_recv()
-
-    widened = saved[...].astype(WIDE)
-    inverse = lax.rsqrt(jnp.mean(widened * widened, axis=-1, keepdims=True) + norm_eps)
-    scaled = dn[...].astype(WIDE) * gain[...]
-    inner_mean = jnp.mean(scaled * widened, axis=-1, keepdims=True)
-    project_grad = inverse * scaled - widened * (inverse * inverse * inverse * inner_mean)
-    grads[...] = up[...] + project_grad.astype(SLIM)
-    back_copy = remote(grads, back, csend.at[1], crecv.at[1], (preceding, me))
-    back_copy.start()
+    pl.when(at_lead_edge)(lambda: finish_block(far))
+
+    pl.when(jnp.logical_not(early))(give_back)
 
     @pl.when(lead)
     def _():
@@ -520,26 +614,39 @@
 
         @pl.when(elsewhere(j))
         def _():
-            for h in range(group):
-                mixed_copy(j, h).wait_send()
-
-    for block in range(n):
-        pl.when(jnp.logical_not(lead))(lambda: mate_sum(block).wait_send())
+            for i in range(len(spans)):
+                mixed_copy(j, i).wait_send()
+
+    @pl.when(trailing)
+    def _():
+        for block, c in each_chunk(*range(n)):
+            mate_sum(block, c).wait_send()
 
     @pl.when(lead)
     def _():
-        partner_sum(partner).wait_send()
-        for block in (near, far):
-            pl.when(at_edge)(lambda: owner_sum(block).wait_send())
-            pl.when(jnp.logical_not(at_edge))(lambda: partner_sum(block).wait_send())
+        for _, c in each_chunk(partner):
+            partner_sum(partner, c).wait_send()
+        for block, c in each_chunk(near, far):
+            pl.when(at_edge)(lambda: owner_sum(block, c).wait_send())
+            pl.when(jnp.logical_not(at_edge))(lambda: partner_sum(block, c).wait_send())
 
     ahead_copy.wait()
-    back_copy.wait()
-
-
-def hand_kernel(first, second, first_out, second_out):
-    first_out[...] = first[...]
-    second_out[...] = second[...]
+    for c in range(len(chunks)):
+        back_copy(c).wait()
+
+
+def hand_kernel(first, second, first_out, second_out, block, sems):
+    takes = [pltpu.make_async_copy(ref, block.at[i], sems.at[i]) for i, ref in enumerate((first, second))]
+    gives = [
+        pltpu.make_async_copy(block.at[i], ref, sems.at[i + 2]) for i, ref in enumerate((first_out, second_out))
+    ]
+    for take in takes:
+        take.start()
+    for take, give in zip(takes, gives):
+        take.wait()
+        give.start()
+    for give in gives:
+        give.wait()
 
 
 def by_pairs(n, sections):
@@ -553,6 +660,8 @@
         group = gq // HEAD_DIM
         wide = gq + keyval_weight.shape[2] // n
 
+        chunks = len(row_chunks(rows))
+
         half_dim = HEAD_DIM // 2
         frequency = rope_base ** (-2.0 * np.arange(half_dim) / HEAD_DIM)
         signs = np.ones(half_dim)
@@ -571,21 +680,22 @@
         ahead, back = pl.pallas_call(
             functools.partial(layer_kernel, n, sections),
             out_shape=pair,
-            in_specs=[VMEM, VMEM, VMEM, VMEM, ANY, ANY, ANY, VMEM, VMEM],
+            in_specs=[ANY] * 9,
             out_specs=(VMEM,) * 2,
             scratch_shapes=[
-                held(2, n, rows, width), held(2, rows, width),
+                *[held(rows, width)] * 3, held(1, width, kind=WIDE), held(1, rows, kind=jnp.int32),
+                held(2, HEAD_DIM, kind=WIDE), held(2, n, rows, width), held(2, rows, width),
                 held(n, rows, gq), held(n, rows, gq), held(query_width, width), held(n, depth, wide),
                 held(n, 1, rows, kind=jnp.int32), held(n * rows, n * rows, kind=WIDE),
                 held(n * rows, HEAD_DIM, kind=WIDE), held(n * rows, HEAD_DIM, kind=WIDE),
                 held(2, n * rows, HEAD_DIM), held(2, n * rows, HEAD_DIM),
                 held(n * rows, HEAD_DIM, kind=WIDE), held(n * rows, HEAD_DIM, kind=WIDE),
-                held(n, group, rows, HEAD_DIM), held(n, group, rows, HEAD_DIM), held(n * rows, wide),
+                held(n, rows, gq), held(n, rows, gq), held(n * rows, wide),
                 held(n, rows, width), held(n, rows, width), held(n, rows, width), held(rows, width),
                 held(rows, width), held(rows, width),
                 dma((2, 2, n)), dma((2, n)), dma((n, group + 2)), dma((n, group + 2)),
-                *[dma((n,))] * 4, *[dma((n, group))] * 2, *[dma((n,))] * 5, dma((1,)),
-                *[dma((2,))] * 2, dma((1,)),
+                *[dma((n,))] * 4, *[dma((n, 2))] * 2, *[dma((n, chunks))] * 5, dma((chunks,)),
+                *[dma((chunks + 1,))] * 2, dma((7,)),
             ],
             compiler_params=pltpu.CompilerParams(
                 collective_id=0, has_side_effects=True, vmem_limit_bytes=60 * 2**20
@@ -596,7 +706,8 @@
             query_weight[0], keyval_weight[0], token_positions[None], waves,
         )
         ahead, back = pl.pallas_call(
-            hand_kernel, out_shape=pair, in_specs=[VMEM] * 2, out_specs=(VMEM,) * 2, name="hand"
+            hand_kernel, out_shape=pair, in_specs=[ANY] * 2, out_specs=(ANY,) * 2,
+            scratch_shapes=[held(2, rows, width), dma((4,))], name="hand",
         )(ahead, back)
         return (ahead[None], back[None])
 
@@ -618,7 +729,9 @@
 
     def chosen(*blocks):
         kv_heads = blocks[6].shape[2] // (2 * HEAD_DIM)
-        if n == 4 and sections > 2 and sections % 2 == 0 and kv_heads == n:
+        rows, query_heads = blocks[0].shape[1], blocks[5].shape[2] // HEAD_DIM
+        paired = n == 4 and sections > 2 and sections % 2 == 0
+        if paired and kv_heads == n and query_heads > n and rows % 16 == 0:
             return by_pairs(n, sections)(*blocks)
         return shards(*blocks)
 

time: 146 us -> 137 us (0.938); the launches traced: 143 us -> 137 us
  Pallas kernels: 142 us -> 136 us
    pallas_call x1, Pallas kernels: 140 us -> 134 us  [step(): pl.pallas_call(functools.partial(layer_kernel, n, sections), out_shape=pa...]
where the time goes in v2:
time: 137 us
  Pallas kernels  136 us (99%)
    pallas_call x1, Pallas kernels, step(): pl.pallas_call(functools.partial(layer_kernel, n, sections), out_shape=pa...  134 us

profile of v2, /device:TPU:0, one launch (start us, length us, event | category | flops | bytes accessed | tf_op | source)
XLA Modules:
  0.0 137.0 jit_solution(7264988027283818121)
XLA Ops:
  0.6 134.2 %layer.1 = (bf16[112,2048]{1,0:T(8,128)(2,1)}, bf16[112,2048]{1,0:T(8,128)(2,1)}) custom-call(bf16[112,2048]{1,0:T(8,128)(2,1)} %bitcast.12, bf16[112,2048]{1,0:T(8,128)(2,1)} %bitcast.13, bf16[112,2048]{1,0:T(8,128)(2,1)} %bitcast.14, f32[1,2048]{1,0:T(1,128)} %gain_hbm.1, bf16[2048,2048]{1,0:T(8,128)(2,1)} %bitcast.9, bf16[512,2048]{1,0:T(8,128)(2,1)} %bitcast.10, ...), custom_call_target="tpu_custom_call" | custom-call | tf_op jit(solution)/shard_map/layer/pallas_call | solution.py:680
  134.8 2.0 %hand.1 = (bf16[112,2048]{1,0:T(8,128)(2,1)}, bf16[112,2048]{1,0:T(8,128)(2,1)}) custom-call(bf16[112,2048]{1,0:T(8,128)(2,1)} %get-tuple-element.6.first, bf16[112,2048]{1,0:T(8,128)(2,1)} %get-tuple-element.7.second), custom_call_target="tpu_custom_call" | custom-call | tf_op jit(solution)/shard_map/hand/pallas_call | solution.py:708

commit v3 on v2

--- a/solution.py
+++ b/solution.py
@@ -164,6 +164,9 @@
     return pltpu.make_async_remote_copy(
         src_ref=src, dst_ref=dst, send_sem=send, recv_sem=recv, device_id=device, device_id_type=MESH
     )
+
+
+HBM = pl.BlockSpec(memory_space=pltpu.HBM)
 
 
 def row_chunks(rows):
@@ -441,8 +444,6 @@
     for h in range(group):
         for j in range(n):
             weight_arrived(j, h)
-        if h == last:
-            send_mixed(0, far, near)
         if h == 0:
             for block in range(n):
                 pl.when(elsewhere(block))(
@@ -459,6 +460,7 @@
 
     dqkv[:, pl.ds(gq, HEAD_DIM)] = turn(dkey[...].astype(SLIM).astype(WIDE), -1.0).astype(SLIM)
     dqkv[:, pl.ds(gq + HEAD_DIM, HEAD_DIM)] = dval[...].astype(SLIM)
+    send_mixed(0, far, near)
 
     def partial_grads(first):
         block_rows = dqkv[pl.ds(pl.multiple_of(first * rows, 16), half * rows), :]
@@ -630,23 +632,12 @@
             pl.when(at_edge)(lambda: owner_sum(block, c).wait_send())
             pl.when(jnp.logical_not(at_edge))(lambda: partner_sum(block, c).wait_send())
 
-    ahead_copy.wait()
+    ahead_copy.wait_send()
     for c in range(len(chunks)):
-        back_copy(c).wait()
-
-
-def hand_kernel(first, second, first_out, second_out, block, sems):
-    takes = [pltpu.make_async_copy(ref, block.at[i], sems.at[i]) for i, ref in enumerate((first, second))]
-    gives = [
-        pltpu.make_async_copy(block.at[i], ref, sems.at[i + 2]) for i, ref in enumerate((first_out, second_out))
-    ]
-    for take in takes:
-        take.start()
-    for take, give in zip(takes, gives):
-        take.wait()
-        give.start()
-    for give in gives:
-        give.wait()
+        back_copy(c).wait_send()
+    ahead_copy.wait_recv()
+    for c in range(len(chunks)):
+        back_copy(c).wait_recv()
 
 
 def by_pairs(n, sections):
@@ -679,8 +670,8 @@
         dma = pltpu.SemaphoreType.DMA
         ahead, back = pl.pallas_call(
             functools.partial(layer_kernel, n, sections),
-            out_shape=pair,
-            in_specs=[ANY] * 9,
+            out_shape=(pltpu.VMEM((rows, width), SLIM),) * 2,
+            in_specs=[HBM] * 9,
             out_specs=(VMEM,) * 2,
             scratch_shapes=[
                 *[held(rows, width)] * 3, held(1, width, kind=WIDE), held(1, rows, kind=jnp.int32),
@@ -698,17 +689,13 @@
                 *[dma((chunks + 1,))] * 2, dma((7,)),
             ],
             compiler_params=pltpu.CompilerParams(
-                collective_id=0, has_side_effects=True, vmem_limit_bytes=60 * 2**20
+                collective_id=0, has_side_effects=True, vmem_limit_bytes=67043328 - 4 * rows * width - 2**16
             ),
             name="layer",
         )(
             section_inputs[0], saved_inputs[0], output_grads[0], norm_gain, output_weight[0],
             query_weight[0], keyval_weight[0], token_positions[None], waves,
         )
-        ahead, back = pl.pallas_call(
-            hand_kernel, out_shape=pair, in_specs=[ANY] * 2, out_specs=(ANY,) * 2,
-            scratch_shapes=[held(2, rows, width), dma((4,))], name="hand",
-        )(ahead, back)
         return (ahead[None], back[None])
 
     return step

time: 137 us -> 133 us (0.971)
  Pallas kernels: 136 us -> 131 us
  local copies, waits for them, and re-layouts: 0 us -> 1.54 us
    pallas_call x2 -> x1, Pallas kernels: 136 us -> 131 us  [step(): pl.pallas_call(functools.partial(layer_kernel, n, sections), out_shape=(p...]
    unnamed x0 -> x2, local copies, waits for them, and re-layouts: none -> 1.54 us
where the time goes in v3:
time: 133 us
  Pallas kernels  131 us (98%)
  local copies, waits for them, and re-layouts  1.54 us (1%)
    pallas_call x1, Pallas kernels, step(): pl.pallas_call(functools.partial(layer_kernel, n, sections), out_shape=(p...  131 us

profile of v3, /device:TPU:0, one launch (start us, length us, event | category | flops | bytes accessed | tf_op | source)
XLA Modules:
  0.0 133.2 jit_solution(11796328224701259442)
XLA Ops:
  0.6 131.0 %layer.1 = (bf16[112,2048]{1,0:T(8,128)(2,1)S(1)}, bf16[112,2048]{1,0:T(8,128)(2,1)S(1)}) custom-call(bf16[112,2048]{1,0:T(8,128)(2,1)} %bitcast.14, bf16[112,2048]{1,0:T(8,128)(2,1)} %bitcast.15, bf16[112,2048]{1,0:T(8,128)(2,1)} %bitcast.16, f32[1,2048]{1,0:T(1,128)} %gain_hbm.1, bf16[2048,2048]{1,0:T(8,128)(2,1)} %bitcast.11, bf16[512,2048]{1,0:T(8,128)(2,1)} %bitcast.12, ...), custom_call_target="tpu_custom_call" | custom-call | tf_op jit(solution)/shard_map/layer/pallas_call | solution.py:671
  131.6 0.8 copy.13
  132.4 0.8 copy.14

commit v4 on v3

--- a/solution.py
+++ b/solution.py
@@ -171,7 +171,9 @@
 
 def row_chunks(rows):
     tiles = rows // 16
-    sizes = [size * 16 for size in ((tiles - 1) - (tiles - 1) // 2, (tiles - 1) // 2, 1) if size]
+    singles = min(tiles, 3)
+    rest = tiles - singles
+    sizes = [size * 16 for size in (rest - rest // 2, rest // 2, *[1] * singles) if size]
     return [(sum(sizes[:i]), size) for i, size in enumerate(sizes)]
 
 
@@ -204,7 +206,6 @@
     total_rows = n * rows
     scale = HEAD_DIM ** (-0.5)
     following, preceding = lax.rem(section + 1, sections), lax.rem(section + sections - 1, sections)
-    pieces = group + 2
 
     barrier = pltpu.get_barrier_semaphore()
     for k in range(1, n):
@@ -247,7 +248,7 @@
         return (base + lax.rem(j, 2), owner_core * half + j // 2)
 
     def token_copy(batch, lane, src, block, device):
-        return remote(src, nx.at[batch, block], nsend.at[batch, lane, block], nrecv.at[batch, block], device)
+        return remote(src, nx.at[batch, block], nsend.at[batch, lane], nrecv.at[batch, block], device)
 
     def to_mate(batch, block):
         return token_copy(batch, 0, nx.at[batch, block], block, (mate, me))
@@ -268,16 +269,22 @@
     def weight_copy(j, piece):
         src, to = piece_source(j, piece)
         return remote(
-            src, wh.at[me, :, pl.ds(to, HEAD_DIM)], wsend.at[j, piece], wrecv.at[me, piece], seat(core, j)
+            src, wh.at[me, :, pl.ds(to, HEAD_DIM)], wsend.at[j], wrecv.at[min(piece, group)], seat(core, j)
         )
 
     def weight_here(j, piece):
         src, to = piece_source(j, piece)
-        return pltpu.make_async_copy(src, wh.at[me, :, pl.ds(to, HEAD_DIM)], wrecv.at[me, piece])
-
-    def weight_arrived(block, piece):
-        dst = wh.at[block, :, pl.ds(piece * HEAD_DIM, HEAD_DIM)]
-        remote(dst, dst, wsend.at[0, 0], wrecv.at[block, piece], (section, me)).wait_recv()
+        return pltpu.make_async_copy(src, wh.at[me, :, pl.ds(to, HEAD_DIM)], wrecv.at[min(piece, group)])
+
+    def taken(dst, recv):
+        remote(dst, dst, osend.at[0], recv, (section, me)).wait_recv()
+
+    def given(src, send):
+        remote(src, src, send, orecv.at[0], (section, me)).wait_send()
+
+    def weight_arrived(piece):
+        size = HEAD_DIM if piece < group else 2 * HEAD_DIM
+        taken(wh.at[:, :, pl.ds(piece * HEAD_DIM, size)], wrecv.at[piece])
 
     def here(j):
         return jnp.logical_and(lead, group_at == j)
@@ -289,10 +296,10 @@
             pl.when(jnp.logical_not(here(j)))(lambda: weight_copy(j, piece).start())
 
     def grad_copy(j):
-        return remote(mgl.at[j], mg.at[me], msend.at[j], mrecv.at[me], seat(core, j))
+        return remote(mgl.at[j], mg.at[me], msend.at[0], mrecv.at[0], seat(core, j))
 
     def place_copy(k):
-        return remote(pos, posg.at[me], psend.at[k], precv.at[me], (section, lax.rem(me + k, n)))
+        return remote(pos, posg.at[me], psend.at[0], precv.at[0], (section, lax.rem(me + k, n)))
 
     @pl.when(lead)
     def _():
@@ -331,7 +338,7 @@
 
     def token_arrived(batch, block):
         dst = nx.at[batch, block]
-        remote(dst, dst, nsend.at[0, 0, 0], nrecv.at[batch, block], (section, me)).wait_recv()
+        remote(dst, dst, nsend.at[0, 0], nrecv.at[batch, block], (section, me)).wait_recv()
 
     @pl.when(lead)
     def _():
@@ -344,9 +351,7 @@
         for piece in range(group):
             send_weights(piece)
 
-    for k in range(1, n):
-        source = lax.rem(me + k, n)
-        remote(pos, posg.at[source], psend.at[0], precv.at[source], (section, me)).wait_recv()
+    taken(posg.at[pl.ds(0, n - 1)], precv.at[0])
     columns = []
     for j in range(n):
         column = jnp.transpose(jnp.broadcast_to(posg[j].astype(WIDE), (HEAD_DIM, rows)))
@@ -379,9 +384,7 @@
             result = term if result is None else result + term
         return result
 
-    for piece in (group, group + 1):
-        for j in range(n):
-            weight_arrived(j, piece)
+    weight_arrived(group)
     for batch in (0, 1):
         both = projected(batch, pl.ds(gq, 2 * HEAD_DIM))
         keys[batch] = turn(both[:, :HEAD_DIM], 1.0).astype(SLIM)
@@ -399,7 +402,7 @@
         at = pl.ds(*spans[i])
         return remote(
             mixed.at[block, :, at], mixed_in.at[group_at, :, at],
-            asend.at[block, i], arecv.at[group_at, i], (served, block),
+            asend.at[i], arecv.at[i], (served, block),
         )
 
     def elsewhere(block):
@@ -442,15 +445,10 @@
     dval[...] = jnp.zeros_like(dval)
 
     for h in range(group):
-        for j in range(n):
-            weight_arrived(j, h)
+        weight_arrived(h)
         if h == 0:
-            for block in range(n):
-                pl.when(elsewhere(block))(
-                    lambda: remote(
-                        mg.at[block], mg.at[block], msend.at[0], mrecv.at[block], (section, me)
-                    ).wait_recv()
-                )
+            pl.when(lead)(lambda: taken(mg.at[pl.ds(0, n - 1)], mrecv.at[0]))
+            pl.when(jnp.logical_not(lead))(lambda: taken(mg, mrecv.at[0]))
         backward_head(h)
         if h < last:
             forward_head(h)
@@ -471,24 +469,21 @@
 
     chunks = row_chunks(rows)
 
-    def mate_sum(block, c):
+    def mate_sum(slot, block):
+        return remote(part.at[block], from_mate.at[block], bsend.at[0], brecv.at[slot], (mate, me))
+
+    def mate_sum_taken(slot, block):
+        taken(from_mate.at[block], brecv.at[slot])
+
+    def partner_sum(slot, block, c):
         at = pl.ds(*chunks[c])
         return remote(
-            part.at[block, at], from_mate.at[block, at], bsend.at[block, c], brecv.at[block, c], (mate, me)
-        )
-
-    def partner_sum(block, c):
-        at = pl.ds(*chunks[c])
-        return remote(
-            part.at[block, at], from_z.at[block, at], zsend.at[block, c], zrecv.at[block, c], (section, partner)
+            part.at[block, at], from_z.at[block, at], zsend.at[0], zrecv.at[slot, c], (section, partner)
         )
 
     def owner_sum(block, c):
         at = pl.ds(*chunks[c])
-        return remote(part.at[block, at], dn.at[at], osend.at[block, c], orecv.at[c], (section, block))
-
-    def each_chunk(*blocks):
-        return [(block, c) for block in blocks for c in range(len(chunks))]
+        return remote(part.at[block, at], dn.at[at], osend.at[0], orecv.at[c], (section, block))
 
     def summed_part(block, c, *others):
         at = pl.ds(*chunks[c])
@@ -505,25 +500,25 @@
 
     @pl.when(trailing)
     def _():
-        for block, c in each_chunk(near, far):
-            mate_sum(block, c).start()
+        mate_sum(0, near).start()
+        mate_sum(1, far).start()
 
     partial_grads(side * half)
 
     @pl.when(trailing)
     def _():
-        for block, c in each_chunk(partner, me):
-            mate_sum(block, c).start()
-
-    def pass_on(block, c):
-        mate_sum(block, c).wait_recv()
-        part[block, pl.ds(*chunks[c])] = summed_part(block, c, from_mate)
-        partner_sum(block, c).start()
+        mate_sum(2, partner).start()
+        mate_sum(3, me).start()
+
+    def pass_on(slot, block):
+        mate_sum_taken(slot, block)
+        for c in range(len(chunks)):
+            part[block, pl.ds(*chunks[c])] = summed_part(block, c, from_mate)
+            partner_sum(slot, block, c).start()
 
     @pl.when(at_lead_inner)
     def _():
-        for block, c in each_chunk(near):
-            pass_on(block, c)
+        pass_on(0, near)
 
     forward_head(last)
     send_mixed(1, far, near, partner, me)
@@ -531,36 +526,35 @@
 
     @pl.when(at_lead_inner)
     def _():
-        for block, c in each_chunk(far, partner):
-            pass_on(block, c)
+        pass_on(1, far)
+        pass_on(2, partner)
 
     @pl.when(at_lead_edge)
     def _():
-        for block, c in each_chunk(partner):
-            pass_on(block, c)
-
-
-    def finish_block(block):
+        pass_on(2, partner)
+
+
+    def finish_block(slot, block):
+        mate_sum_taken(slot, block)
         for c in range(len(chunks)):
-            mate_sum(block, c).wait_recv()
-            partner_sum(block, c).wait_recv()
+            partner_sum(slot, block, c).wait_recv()
             part[block, pl.ds(*chunks[c])] = summed_part(block, c, from_mate, from_z)
             owner_sum(block, c).start()
 
-    pl.when(at_lead_edge)(lambda: finish_block(near))
+    pl.when(at_lead_edge)(lambda: finish_block(0, near))
 
     def back_copy(c):
         at = pl.ds(*chunks[c])
-        return remote(grads.at[at], back.at[at], csend.at[c], crecv.at[c], (preceding, me))
+        return remote(grads.at[at], back.at[at], csend.at[1], crecv.at[1], (preceding, me))
 
     def give_back():
+        pl.when(lead)(lambda: mate_sum_taken(3, me))
         for c, chunk in enumerate(chunks):
             at = pl.ds(*chunk)
 
             @pl.when(lead)
             def _():
-                mate_sum(me, c).wait_recv()
-                partner_sum(me, c).wait_recv()
+                partner_sum(2, me, c).wait_recv()
                 dn[at] = summed_part(me, c, from_mate, from_z)
 
             pl.when(trailing)(lambda: owner_sum(me, c).wait_recv())
@@ -576,68 +570,57 @@
     pl.when(early)(give_back)
 
     total = tokens[...].astype(WIDE)
+    for i, span in enumerate(spans):
+        at = pl.ds(*span)
+        pl.when(lead)(lambda: taken(mixed_in.at[pl.ds(0, n - 1), :, at], arecv.at[i]))
+        pl.when(trailing)(lambda: taken(mixed_in.at[:, :, at], arecv.at[i]))
     for j in range(n):
-        def arrived():
-            for i, span in enumerate(spans):
-                dst = mixed_in.at[j, :, pl.ds(*span)]
-                remote(dst, dst, asend.at[0, 0], arecv.at[j, i], (section, me)).wait_recv()
-
-        pl.when(jnp.logical_not(here(j)))(arrived)
         total += jnp.dot(mixed_in[j], wo[pl.ds(j * gq, gq), :], preferred_element_type=WIDE)
     produced[...] = total.astype(SLIM)
-    ahead_copy = remote(produced, ahead, csend.at[len(chunks)], crecv.at[len(chunks)], (following, me))
+    ahead_copy = remote(produced, ahead, csend.at[0], crecv.at[0], (following, me))
     ahead_copy.start()
-    pl.when(at_lead_edge)(lambda: finish_block(far))
+    pl.when(at_lead_edge)(lambda: finish_block(1, far))
 
     pl.when(jnp.logical_not(early))(give_back)
 
     @pl.when(lead)
     def _():
         for batch in (0, 1):
-            for block in range(n):
-                to_mate(batch, block).wait_send()
-            to_partner(batch, me).wait_send()
-            for block in (near, far):
-                pl.when(at_edge)(lambda: to_partner(batch, block).wait_send())
-
-    @pl.when(jnp.logical_not(lead))
-    def _():
-        for batch in (0, 1):
-            to_edge(batch).wait_send()
-
-    for k in range(1, n):
-        place_copy(k).wait_send()
+            given(nx.at[batch], nsend.at[batch, 0])
+        given(mgl.at[pl.ds(0, n - 1)], msend.at[0])
+        for i, span in enumerate(spans):
+            given(mixed.at[pl.ds(0, n - 1), :, pl.ds(*span)], asend.at[i])
+
+    @pl.when(at_lead_edge)
+    def _():
+        for batch in (0, 1):
+            given(nx.at[batch, pl.ds(0, half + 1)], nsend.at[batch, 1])
+        given(part.at[0], zsend.at[0])
+        given(part.at[pl.ds(0, half)], osend.at[0])
+
+    @pl.when(at_lead_inner)
+    def _():
+        for batch in (0, 1):
+            given(nx.at[batch, 0], nsend.at[batch, 1])
+        given(part.at[pl.ds(0, half + 1)], zsend.at[0])
+
+    @pl.when(trailing)
+    def _():
+        for batch in (0, 1):
+            given(mine.at[batch], nsend.at[batch, 0])
+        given(mgl, msend.at[0])
+        for i, span in enumerate(spans):
+            given(mixed.at[:, :, pl.ds(*span)], asend.at[i])
+        given(part, bsend.at[0])
+
+    given(posg.at[pl.ds(0, n - 1)], psend.at[0])
     for j in range(n):
-        @pl.when(jnp.logical_not(here(j)))
-        def _():
-            for piece in range(pieces):
-                weight_copy(j, piece).wait_send()
-            grad_copy(j).wait_send()
-
-        @pl.when(elsewhere(j))
-        def _():
-            for i in range(len(spans)):
-                mixed_copy(j, i).wait_send()
-
-    @pl.when(trailing)
-    def _():
-        for block, c in each_chunk(*range(n)):
-            mate_sum(block, c).wait_send()
-
-    @pl.when(lead)
-    def _():
-        for _, c in each_chunk(partner):
-            partner_sum(partner, c).wait_send()
-        for block, c in each_chunk(near, far):
-            pl.when(at_edge)(lambda: owner_sum(block, c).wait_send())
-            pl.when(jnp.logical_not(at_edge))(lambda: partner_sum(block, c).wait_send())
+        pl.when(jnp.logical_not(here(j)))(lambda: given(wh.at[0], wsend.at[j]))
 
     ahead_copy.wait_send()
-    for c in range(len(chunks)):
-        back_copy(c).wait_send()
+    given(grads, csend.at[1])
     ahead_copy.wait_recv()
-    for c in range(len(chunks)):
-        back_copy(c).wait_recv()
+    taken(back, crecv.at[1])
 
 
 def by_pairs(n, sections):
@@ -684,9 +667,9 @@
                 held(n, rows, gq), held(n, rows, gq), held(n * rows, wide),
                 held(n, rows, width), held(n, rows, width), held(n, rows, width), held(rows, width),
                 held(rows, width), held(rows, width),
-                dma((2, 2, n)), dma((2, n)), dma((n, group + 2)), dma((n, group + 2)),
-                *[dma((n,))] * 4, *[dma((n, 2))] * 2, *[dma((n, chunks))] * 5, dma((chunks,)),
-                *[dma((chunks + 1,))] * 2, dma((7,)),
+                dma((2, 2)), dma((2, n)), dma((n,)), dma((group + 1,)), *[dma((1,))] * 4, *[dma((2,))] * 2,
+                dma((1,)), dma((n,)), dma((1,)), dma((3, chunks)), dma((1,)), dma((chunks,)),
+                *[dma((2,))] * 2, dma((7,)),
             ],
             compiler_params=pltpu.CompilerParams(
                 collective_id=0, has_side_effects=True, vmem_limit_bytes=67043328 - 4 * rows * width - 2**16

time: 133 us -> 132 us (level)
  no operation moved by 1% of the time
where the time goes in v4:
time: 132 us
  Pallas kernels  130 us (98%)
  local copies, waits for them, and re-layouts  1.54 us (1%)
    pallas_call x1, Pallas kernels, step(): pl.pallas_call(functools.partial(layer_kernel, n, sections), out_shape=(p...  130 us

profile of v4, /device:TPU:0, one launch (start us, length us, event | category | flops | bytes accessed | tf_op | source)
XLA Modules:
  0.0 131.9 jit_solution(17342793082264786806)
XLA Ops:
  0.6 129.7 %layer.1 = (bf16[112,2048]{1,0:T(8,128)(2,1)S(1)}, bf16[112,2048]{1,0:T(8,128)(2,1)S(1)}) custom-call(bf16[112,2048]{1,0:T(8,128)(2,1)} %bitcast.14, bf16[112,2048]{1,0:T(8,128)(2,1)} %bitcast.15, bf16[112,2048]{1,0:T(8,128)(2,1)} %bitcast.16, f32[1,2048]{1,0:T(1,128)} %gain_hbm.1, bf16[2048,2048]{1,0:T(8,128)(2,1)} %bitcast.11, bf16[512,2048]{1,0:T(8,128)(2,1)} %bitcast.12, ...), custom_call_target="tpu_custom_call" | custom-call | tf_op jit(solution)/shard_map/layer/pallas_call | solution.py:654
  130.4 0.8 copy.13
  131.1 0.8 copy.14

commit v5 on v4

--- a/solution.py
+++ b/solution.py
@@ -266,15 +266,20 @@
         start = (piece - group) * kv_half + j * HEAD_DIM
         return wkv.at[:, pl.ds(pl.multiple_of(start, HEAD_DIM), HEAD_DIM)], piece * HEAD_DIM
 
+    def piece_slot(piece):
+        if piece != group - 1:
+            return min(piece, group)
+        return jnp.where(me == half - core, group + 1, piece)
+
     def weight_copy(j, piece):
         src, to = piece_source(j, piece)
         return remote(
-            src, wh.at[me, :, pl.ds(to, HEAD_DIM)], wsend.at[j], wrecv.at[min(piece, group)], seat(core, j)
+            src, wh.at[me, :, pl.ds(to, HEAD_DIM)], wsend.at[j], wrecv.at[piece_slot(piece)], seat(core, j)
         )
 
     def weight_here(j, piece):
         src, to = piece_source(j, piece)
-        return pltpu.make_async_copy(src, wh.at[me, :, pl.ds(to, HEAD_DIM)], wrecv.at[min(piece, group)])
+        return pltpu.make_async_copy(src, wh.at[me, :, pl.ds(to, HEAD_DIM)], wrecv.at[piece_slot(piece)])
 
     def taken(dst, recv):
         remote(dst, dst, osend.at[0], recv, (section, me)).wait_recv()
@@ -375,12 +380,11 @@
     def dot(a, b, dims):
         return lax.dot_general(a, b, (dims, ((), ())), preferred_element_type=WIDE)
 
-    def projected(batch, at):
+    def projected(batch, at, sources=range(n)):
         result = None
-        for j in range(n):
-            term = dot(
-                nx[batch, :, :, pl.ds(j * depth, depth)].reshape(total_rows, depth), wh[j, :, at], ((1,), (0,))
-            )
+        for j in sources:
+            columns = pl.ds(pl.multiple_of(j * depth, HEAD_DIM), depth)
+            term = dot(nx[batch, :, :, columns].reshape(total_rows, depth), wh[j, :, at], ((1,), (0,)))
             result = term if result is None else result + term
         return result
 
@@ -427,7 +431,15 @@
 
     def backward_head(h):
         at = pl.ds(h * HEAD_DIM, HEAD_DIM)
-        queries = turn(projected(1, at), 1.0).astype(SLIM)
+        if h < last:
+            weight_arrived(h)
+            result = projected(1, at)
+        else:
+            taken(wh.at[pl.ds(0, n - 1), :, at], wrecv.at[h])
+            result = projected(1, at, [lax.rem(near + i, n) for i in range(1, n)])
+            taken(wh.at[0, :, at], wrecv.at[group + 1])
+            result += projected(1, at, [near])
+        queries = turn(result, 1.0).astype(SLIM)
         numerators, totals = weigh(queries, keys[1])
         rounded = numerators.astype(SLIM)
         summed = dot(rounded, values[1], ((1,), (0,)))
@@ -445,7 +457,6 @@
     dval[...] = jnp.zeros_like(dval)
 
     for h in range(group):
-        weight_arrived(h)
         if h == 0:
             pl.when(lead)(lambda: taken(mg.at[pl.ds(0, n - 1)], mrecv.at[0]))
             pl.when(jnp.logical_not(lead))(lambda: taken(mg, mrecv.at[0]))
@@ -496,19 +507,23 @@
     at_lead_edge = jnp.logical_and(lead, at_edge)
     at_lead_inner = jnp.logical_and(lead, jnp.logical_not(at_edge))
 
-    partial_grads((1 - side) * half)
-
-    @pl.when(trailing)
-    def _():
+    def send_outer():
         mate_sum(0, near).start()
         mate_sum(1, far).start()
 
-    partial_grads(side * half)
-
-    @pl.when(trailing)
-    def _():
+    def send_inner():
         mate_sum(2, partner).start()
         mate_sum(3, me).start()
+
+    own_first = jnp.where(at_edge, side, 1 - side)
+    trail_edge = jnp.logical_and(trailing, at_edge)
+    trail_inner = jnp.logical_and(trailing, jnp.logical_not(at_edge))
+    partial_grads(own_first * half)
+    pl.when(trail_edge)(send_inner)
+    pl.when(trail_inner)(send_outer)
+    partial_grads((1 - own_first) * half)
+    pl.when(trail_edge)(send_outer)
+    pl.when(trail_inner)(send_inner)
 
     def pass_on(slot, block):
         mate_sum_taken(slot, block)
@@ -570,12 +585,14 @@
     pl.when(early)(give_back)
 
     total = tokens[...].astype(WIDE)
-    for i, span in enumerate(spans):
-        at = pl.ds(*span)
+    for i, (start, size) in enumerate(spans):
+        at = pl.ds(start, size)
         pl.when(lead)(lambda: taken(mixed_in.at[pl.ds(0, n - 1), :, at], arecv.at[i]))
         pl.when(trailing)(lambda: taken(mixed_in.at[:, :, at], arecv.at[i]))
-    for j in range(n):
-        total += jnp.dot(mixed_in[j], wo[pl.ds(j * gq, gq), :], preferred_element_type=WIDE)
+        for j in range(n):
+            total += jnp.dot(
+                mixed_in[j, :, at], wo[pl.ds(j * gq + start, size), :], preferred_element_type=WIDE
+            )
     produced[...] = total.astype(SLIM)
     ahead_copy = remote(produced, ahead, csend.at[0], crecv.at[0], (following, me))
     ahead_copy.start()
@@ -621,6 +638,17 @@
     given(grads, csend.at[1])
     ahead_copy.wait_recv()
     taken(back, crecv.at[1])
+
+
+def hand_kernel(first, second, first_out, second_out, sems):
+    gives = [
+        pltpu.make_async_copy(src, dst, sems.at[i])
+        for i, (src, dst) in enumerate(((first, first_out), (second, second_out)))
+    ]
+    for give in gives:
+        give.start()
+    for give in gives:
+        give.wait()
 
 
 def by_pairs(n, sections):
@@ -667,7 +695,7 @@
                 held(n, rows, gq), held(n, rows, gq), held(n * rows, wide),
                 held(n, rows, width), held(n, rows, width), held(n, rows, width), held(rows, width),
                 held(rows, width), held(rows, width),
-                dma((2, 2)), dma((2, n)), dma((n,)), dma((group + 1,)), *[dma((1,))] * 4, *[dma((2,))] * 2,
+                dma((2, 2)), dma((2, n)), dma((n,)), dma((group + 2,)), *[dma((1,))] * 4, *[dma((2,))] * 2,
                 dma((1,)), dma((n,)), dma((1,)), dma((3, chunks)), dma((1,)), dma((chunks,)),
                 *[dma((2,))] * 2, dma((7,)),
             ],
@@ -679,6 +707,11 @@
             section_inputs[0], saved_inputs[0], output_grads[0], norm_gain, output_weight[0],
             query_weight[0], keyval_weight[0], token_positions[None], waves,
         )
+        ahead, back = (pltpu.with_memory_space_constraint(block, pltpu.VMEM) for block in (ahead, back))
+        ahead, back = pl.pallas_call(
+            hand_kernel, out_shape=pair, in_specs=[VMEM] * 2, out_specs=(HBM,) * 2,
+            scratch_shapes=[dma((2,))], name="hand",
+        )(ahead, back)
         return (ahead[None], back[None])
 
     return step

time: 132 us -> 131 us (level)
  local copies, waits for them, and re-layouts: 1.54 us -> 0 us
    unnamed x2 -> x0, local copies, waits for them, and re-layouts: 1.54 us -> none
where the time goes in v5:
time: 131 us; the launch traced here: 130 us
  Pallas kernels  130 us (99%)
    pallas_call x1, Pallas kernels, step(): pl.pallas_call(functools.partial(layer_kernel, n, sections), out_shape=(p...  129 us

profile of v5, /device:TPU:0, one launch (start us, length us, event | category | flops | bytes accessed | tf_op | source)
XLA Modules:
  0.0 130.4 jit_solution(2380906625152826981)
XLA Ops:
  0.6 128.7 %layer.1 = (bf16[112,2048]{1,0:T(8,128)(2,1)S(1)}, bf16[112,2048]{1,0:T(8,128)(2,1)S(1)}) custom-call(bf16[112,2048]{1,0:T(8,128)(2,1)} %bitcast.12, bf16[112,2048]{1,0:T(8,128)(2,1)} %bitcast.13, bf16[112,2048]{1,0:T(8,128)(2,1)} %bitcast.14, f32[1,2048]{1,0:T(1,128)} %gain_hbm.1, bf16[2048,2048]{1,0:T(8,128)(2,1)} %bitcast.9, bf16[512,2048]{1,0:T(8,128)(2,1)} %bitcast.10, ...), custom_call_target="tpu_custom_call" | custom-call | tf_op jit(solution)/shard_map/layer/pallas_call | solution.py:682
  129.3 0.9 hand.1

commit v6 on v5

--- a/solution.py
+++ b/solution.py
@@ -170,11 +170,7 @@
 
 
 def row_chunks(rows):
-    tiles = rows // 16
-    singles = min(tiles, 3)
-    rest = tiles - singles
-    sizes = [size * 16 for size in (rest - rest // 2, rest // 2, *[1] * singles) if size]
-    return [(sum(sizes[:i]), size) for i, size in enumerate(sizes)]
+    return [(start, 16) for start in range(0, rows, 16)]
 
 
 def layer_kernel(
@@ -515,25 +511,24 @@
         mate_sum(2, partner).start()
         mate_sum(3, me).start()
 
+    def pass_on(slot, block):
+        mate_sum_taken(slot, block)
+        for c in range(len(chunks)):
+            part[block, pl.ds(*chunks[c])] = summed_part(block, c, from_mate)
+            partner_sum(slot, block, c).start()
+
     own_first = jnp.where(at_edge, side, 1 - side)
     trail_edge = jnp.logical_and(trailing, at_edge)
     trail_inner = jnp.logical_and(trailing, jnp.logical_not(at_edge))
     partial_grads(own_first * half)
     pl.when(trail_edge)(send_inner)
     pl.when(trail_inner)(send_outer)
+    pl.when(jnp.logical_and(at_lead_inner, core == 1))(lambda: pass_on(0, near))
     partial_grads((1 - own_first) * half)
     pl.when(trail_edge)(send_outer)
     pl.when(trail_inner)(send_inner)
 
-    def pass_on(slot, block):
-        mate_sum_taken(slot, block)
-        for c in range(len(chunks)):
-            part[block, pl.ds(*chunks[c])] = summed_part(block, c, from_mate)
-            partner_sum(slot, block, c).start()
-
-    @pl.when(at_lead_inner)
-    def _():
-        pass_on(0, near)
+    pl.when(jnp.logical_and(at_lead_inner, core == 0))(lambda: pass_on(0, near))
 
     forward_head(last)
     send_mixed(1, far, near, partner, me)

time: 131 us -> 130 us (level)
  no operation moved by 1% of the time
where the time goes in v6:
time: 130 us
  Pallas kernels  129 us (99%)
    pallas_call x1, Pallas kernels, step(): pl.pallas_call(functools.partial(layer_kernel, n, sections), out_shape=(p...  128 us

profile of v6, /device:TPU:0, one launch (start us, length us, event | category | flops | bytes accessed | tf_op | source)
XLA Modules:
  0.0 129.7 jit_solution(10001791215322206322)
XLA Ops:
  0.6 128.0 %layer.1 = (bf16[112,2048]{1,0:T(8,128)(2,1)S(1)}, bf16[112,2048]{1,0:T(8,128)(2,1)S(1)}) custom-call(bf16[112,2048]{1,0:T(8,128)(2,1)} %bitcast.12, bf16[112,2048]{1,0:T(8,128)(2,1)} %bitcast.13, bf16[112,2048]{1,0:T(8,128)(2,1)} %bitcast.14, f32[1,2048]{1,0:T(1,128)} %gain_hbm.1, bf16[2048,2048]{1,0:T(8,128)(2,1)} %bitcast.9, bf16[512,2048]{1,0:T(8,128)(2,1)} %bitcast.10, ...), custom_call_target="tpu_custom_call" | custom-call | tf_op jit(solution)/shard_map/layer/pallas_call | solution.py:677
  128.6 0.9 hand.1

commit v7 on v6

--- a/solution.py
+++ b/solution.py
@@ -465,7 +465,8 @@
 
     dqkv[:, pl.ds(gq, HEAD_DIM)] = turn(dkey[...].astype(SLIM).astype(WIDE), -1.0).astype(SLIM)
     dqkv[:, pl.ds(gq + HEAD_DIM, HEAD_DIM)] = dval[...].astype(SLIM)
-    send_mixed(0, far, near)
+    holds = jnp.logical_and(jnp.logical_and(lead, core == 0), jnp.logical_not(at_edge))
+    pl.when(jnp.logical_not(holds))(lambda: send_mixed(0, far, near))
 
     def partial_grads(first):
         block_rows = dqkv[pl.ds(pl.multiple_of(first * rows, 16), half * rows), :]
@@ -528,7 +529,10 @@
     pl.when(trail_edge)(send_outer)
     pl.when(trail_inner)(send_inner)
 
-    pl.when(jnp.logical_and(at_lead_inner, core == 0))(lambda: pass_on(0, near))
+    @pl.when(holds)
+    def _():
+        pass_on(0, near)
+        send_mixed(0, far, near)
 
     forward_head(last)
     send_mixed(1, far, near, partner, me)

time: 130 us -> 132 us (1.015); the launches traced: 130 us -> 130 us
  no operation moved by 1% of the time
where the time goes in v7:
time: 132 us; the launch traced here: 130 us
  Pallas kernels  129 us (98%)
    pallas_call x1, Pallas kernels, step(): pl.pallas_call(functools.partial(layer_kernel, n, sections), out_shape=(p...  128 us

profile of v7, /device:TPU:0, one launch (start us, length us, event | category | flops | bytes accessed | tf_op | source)
XLA Modules:
  0.0 129.9 jit_solution(5554549771243573571)
XLA Ops:
  0.6 128.1 %layer.1 = (bf16[112,2048]{1,0:T(8,128)(2,1)S(1)}, bf16[112,2048]{1,0:T(8,128)(2,1)S(1)}) custom-call(bf16[112,2048]{1,0:T(8,128)(2,1)} %bitcast.12, bf16[112,2048]{1,0:T(8,128)(2,1)} %bitcast.13, bf16[112,2048]{1,0:T(8,128)(2,1)} %bitcast.14, f32[1,2048]{1,0:T(1,128)} %gain_hbm.1, bf16[2048,2048]{1,0:T(8,128)(2,1)} %bitcast.9, bf16[512,2048]{1,0:T(8,128)(2,1)} %bitcast.10, ...), custom_call_target="tpu_custom_call" | custom-call | tf_op jit(solution)/shard_map/layer/pallas_call | solution.py:681
  128.8 0.9 hand.1
